TPU v7x, 8 devices: a whole 2x2x1 slice. The times are simulated.
8 devices in a mesh: dp: 2 (over z, y), fsdp: 4 (over x, core).
Axes of the slice: x: 2, y: 2, z: 1, core: 2. Of those that a mesh axis runs over, the one named last changes fastest.
Arguments:
- g_layer: float32 [8, 6, 256, 3072], P(('dp', 'fsdp'))
- g_down: float32 [8, 256, 8192], P(('dp', 'fsdp'))
- g_norm: float32 [8, 4, 3072], P(('dp', 'fsdp'))
- g_embed: float32 [8, 256, 3072], P(('dp', 'fsdp'))
- layer_w: float32 [6, 256, 3072], P(None, 'fsdp')
- layer_m: float32 [6, 256, 3072], P(None, 'fsdp')
- layer_v: float32 [6, 256, 3072], P(None, 'fsdp')
- down_w: float32 [256, 8192], P('fsdp')
- down_m: float32 [256, 8192], P('fsdp')
- down_v: float32 [256, 8192], P('fsdp')
- norm_w: float32 [4, 3072], P(None, 'fsdp')
- norm_m: float32 [4, 3072], P(None, 'fsdp')
- norm_v: float32 [4, 3072], P(None, 'fsdp')
- embed_w: float32 [256, 3072], P('fsdp')
- embed_m: float32 [256, 3072], P('fsdp')
- embed_v: float32 [256, 3072], P('fsdp')
Outputs:
- output 1: float32 [6, 256, 3072], P(None, 'fsdp')
- output 2: float32 [6, 256, 3072], P(None, 'fsdp')
- output 3: float32 [6, 256, 3072], P(None, 'fsdp')
- output 4: bfloat16 [6, 256, 3072], P(None, 'fsdp')
- output 5: float32 [256, 8192], P('fsdp')
- output 6: float32 [256, 8192], P('fsdp')
- output 7: float32 [256, 8192], P('fsdp')
- output 8: bfloat16 [256, 8192], P('fsdp')
- output 9: float32 [4, 3072], P(None, 'fsdp')
- output 10: float32 [4, 3072], P(None, 'fsdp')
- output 11: float32 [4, 3072], P(None, 'fsdp')
- output 12: bfloat16 [4, 3072], P(None, 'fsdp')
- output 13: float32 [256, 3072], P('fsdp')
- output 14: float32 [256, 3072], P('fsdp')
- output 15: float32 [256, 3072], P('fsdp')
- output 16: bfloat16 [256, 3072], P('fsdp')
All inputs are finite; a program needn't handle non-finite values.
Results may differ from a plain program's by a relative error of at most 0.001.
Values sent between devices are 32-bit elements.
A program may use at most 1 GiB of HBM per device.

v0:
```python
import jax
import jax.numpy as jnp
from jax import lax
from jax.sharding import PartitionSpec as P, NamedSharding

ADAM_BETA1 = 0.9
ADAM_BETA2 = 0.95
ADAM_EPS = 1e-8
LEARN_RATE = 4e-4
WEIGHT_DECAY = 0.1
CLIP_EPS = 1e-6
OPT_STEP = 20
BIAS_ONE = 1.0 - ADAM_BETA1 ** OPT_STEP
BIAS_TWO = 1.0 - ADAM_BETA2 ** OPT_STEP


def adamw_step(grad_mean, master, exp_avg, exp_avg_sq, clip_coef, decay_rate):
    clipped = clip_coef * grad_mean
    avg_new = ADAM_BETA1 * exp_avg + (1.0 - ADAM_BETA1) * clipped
    sq_new = ADAM_BETA2 * exp_avg_sq + (1.0 - ADAM_BETA2) * clipped * clipped
    step_dir = (avg_new / BIAS_ONE) / (jnp.sqrt(sq_new / BIAS_TWO) + ADAM_EPS)
    master_new = master - LEARN_RATE * (step_dir + decay_rate * master)
    return master_new, avg_new, sq_new, master_new.astype(jnp.bfloat16)


def solution(mesh):
    dev_count = mesh.shape["dp"] * mesh.shape["fsdp"]
    grad_four = P(("dp", "fsdp"), None, None, None)
    grad_three = P(("dp", "fsdp"), None, None)
    layer_spec = P(None, "fsdp", None)
    down_spec = P("fsdp", None)
    norm_spec = P(None, "fsdp")
    embed_spec = P("fsdp", None)

    def local_update(g_layer, g_down, g_norm, g_embed, layer_w, layer_m, layer_v, down_w, down_m, down_v, norm_w, norm_m, norm_v, embed_w, embed_m, embed_v):
        layer_part = lax.psum_scatter(g_layer[0], "fsdp", scatter_dimension=1, tiled=True)
        down_part = lax.psum_scatter(g_down[0], "fsdp", scatter_dimension=0, tiled=True)
        norm_part = lax.psum_scatter(g_norm[0], "fsdp", scatter_dimension=1, tiled=True)
        embed_part = lax.psum_scatter(g_embed[0], "fsdp", scatter_dimension=0, tiled=True)
        layer_mean = lax.psum(layer_part, "dp") / dev_count
        down_mean = lax.psum(down_part, "dp") / dev_count
        norm_mean = lax.psum(norm_part, "dp") / dev_count
        embed_mean = lax.psum(embed_part, "dp") / dev_count
        local_sq = (jnp.sum(layer_mean * layer_mean) + jnp.sum(down_mean * down_mean)
                    + jnp.sum(norm_mean * norm_mean) + jnp.sum(embed_mean * embed_mean))
        global_norm = jnp.sqrt(lax.psum(local_sq, "fsdp"))
        clip_coef = jnp.minimum(1.0, 1.0 / (global_norm + CLIP_EPS))
        return (adamw_step(layer_mean, layer_w, layer_m, layer_v, clip_coef, WEIGHT_DECAY)
                + adamw_step(down_mean, down_w, down_m, down_v, clip_coef, WEIGHT_DECAY)
                + adamw_step(norm_mean, norm_w, norm_m, norm_v, clip_coef, WEIGHT_DECAY)
                + adamw_step(embed_mean, embed_w, embed_m, embed_v, clip_coef, 0.0))

    in_specs = (grad_four, grad_three, grad_three, grad_three,
                layer_spec, layer_spec, layer_spec, down_spec, down_spec, down_spec,
                norm_spec, norm_spec, norm_spec, embed_spec, embed_spec, embed_spec)
    out_specs = (layer_spec,) * 4 + (down_spec,) * 4 + (norm_spec,) * 4 + (embed_spec,) * 4
    return jax.shard_map(local_update, mesh=mesh, in_specs=in_specs, out_specs=out_specs, check_vma=False)
```

profile of v0, /device:TPU:0, one launch (start us, length us, event | category | flops | bytes accessed | tf_op | source)
XLA Modules:
  0.0 493.8 jit_solution(9411254487424962654)
XLA Ops:
  7.2 0.0 reduce-scatter.11.cloned.1.call-start
  7.2 0.7 reduce-scatter.11.cloned.1.call-update
  7.9 0.0 reduce-scatter.9.cloned.1.call-start
  8.0 0.7 reduce-scatter.9.cloned.1.call-update
  8.7 0.0 reduce-scatter.7.cloned.1.call-start
  8.7 0.0 copy-start.8
  8.7 0.7 reduce-scatter.7.cloned.1.call-update
  9.4 0.0 reduce-scatter.13.cloned.1.call-start
  9.4 0.1 copy-done.8
  9.5 1.7 copy.32
  11.2 0.0 reduce-scatter.13.cloned.1.call-update
  11.2 0.0 all-reduce.3.cloned.1.call-start
  11.2 34.0 %reduce-scatter.11.cloned.1.call-done = f32[64,3072]{1,0:T(8,128)} async-done(((f32[256,3072]{1,0:T(8,128)}), f32[64,3072]{1,0:T(8,128)}) %reduce-scatter.11.cloned.1.call-update) | async-done | bytes 786448 | tf_op jit(solution)/shard_map/reduce_scatter | solution.py:39
  45.3 67.7 %reduce-scatter.9.cloned.1.call-done = f32[64,8192]{1,0:T(8,128)} async-done(((f32[256,8192]{1,0:T(8,128)}), f32[64,8192]{1,0:T(8,128)}) %reduce-scatter.9.cloned.1.call-update) | async-done | bytes 2097168 | tf_op jit(solution)/shard_map/reduce_scatter | solution.py:37
  112.9 134.0 %reduce-scatter.7.cloned.1.call-done = f32[6,64,3072]{2,1,0:T(8,128)} async-done(((f32[6,256,3072]{2,1,0:T(8,128)}), f32[6,64,3072]{2,1,0:T(8,128)}) %reduce-scatter.7.cloned.1.call-update) | async-done | bytes 4718608 | tf_op jit(solution)/shard_map/reduce_scatter | solution.py:36
  247.0 0.0 all-reduce.3.cloned.1.call-update
  247.0 25.3 %reduce-scatter.13.cloned.1.call-done = f32[768,4]{1,0:T(8,128)} async-done(((f32[3072,4]{1,0:T(8,128)}), f32[768,4]{1,0:T(8,128)}) %reduce-scatter.13.cloned.1.call-update) | async-done | bytes 12304
  272.3 1.1 copy.33
  273.4 8.3 %psum.37 = f32[4,768]{1,0:T(4,128)S(1)} all-reduce(f32[4,768]{1,0:T(4,128)S(1)} %copy.33), channel_id=1, replica_groups=mesh['dp'=2,'fsdp'=4] {'dp'}, use_global_device_ids=true, to_apply=%region_7.0 | all-reduce | flops 3072 | bytes 24576 | tf_op jit(solution)/shard_map/psum | solution.py:42
  281.7 0.6 multiply_reduce_fusion.3
  282.3 168.2 %all-reduce.3.cloned.1.call-done = (f32[6,64,3072]{2,1,0:T(8,128)}, f32[64,8192]{1,0:T(8,128)}, f32[64,3072]{1,0:T(8,128)}) async-done(((f32[6,64,3072]{2,1,0:T(8,128)}, f32[64,8192]{1,0:T(8,128)}, f32[64,3072]{1,0:T(8,128)}), (f32[6,64,3072]{2,1,0:T(8,128)}, f32[64,8192]{1,0:T(8,128)}, f32[64,3072]{1,0:T(8,128)})) %all-reduce.3.cloned.1.call-update) | async-done | bytes 7602192 | tf_op jit(solution)/shard_map/psum | solution.py:40
  450.6 0.0 copy-start
  450.6 0.0 copy-start.1
  450.6 4.3 multiply_reduce_fusion
  454.9 0.0 copy-done
  454.9 1.1 multiply_reduce_fusion.1
  456.0 0.0 copy-done.1
  456.0 0.8 multiply_reduce_fusion.2
  459.4 6.8 %psum.39 = f32[]{:T(128)} all-reduce(f32[]{:T(128)S(6)} %add.92), channel_id=1, replica_groups=mesh['dp'=2,'fsdp'=4] {'fsdp'}, use_global_device_ids=true, to_apply=%region_12.0 | all-reduce | flops 1 | bytes 8 | tf_op jit(solution)/shard_map/psum | solution.py:46
  467.0 0.0 copy-start.2
  467.0 0.0 copy-start.3
  467.0 0.0 copy-start.4
  467.0 13.1 %fusion.10 = (bf16[6,64,3072]{2,1,0:T(8,128)(2,1)}, f32[6,64,3072]{2,1,0:T(8,128)}, f32[6,64,3072]{2,1,0:T(8,128)}, f32[6,64,3072]{2,1,0:T(8,128)}) fusion(f32[6,64,3072]{2,1,0:T(8,128)} %param.20, f32[6,64,3072]{2,1,0:T(8,128)} %get-tuple-element.16, f32[]{:T(128)S(6)} %mul.182, f32[6,64,3072]{2,1,0:T(8,128)} %param.21, f32[6,64,3072]{2,1,0:T(8,128)} %param.22), kind=kLoop, calls=%fused_computation.23 | loop fusion | flops 20054016 | bytes 35389444 | tf_op jit(solution)/shard_map/convert_element_type | solution.py:23
  480.0 0.0 copy-done.2
  480.1 0.0 copy-done.3
  480.1 0.4 copy-done.4
  480.5 4.2 fusion.8
  484.7 0.0 copy-done.5
  484.7 0.0 copy-done.6
  484.7 0.0 copy-done.7
  484.7 0.0 copy-start.9
  484.7 0.0 copy-start.10
  484.7 0.0 copy-start.11
  484.7 1.9 fusion.4
  486.6 0.0 copy-done.9
  486.6 0.0 copy-done.10
  486.7 0.0 copy-done.11
  486.7 0.6 fusion.6
  (3 shorter events, 0.0 us)
Async XLA Ops:
  7.2 38.1 %reduce-scatter.11.cloned.1.call-start = ((), (), s32[]{:S(2)}) async-start(), calls=%async_computation.6 | async-start | bytes 3932160 | tf_op jit(solution)/shard_map/reduce_scatter | solution.py:39
  7.9 105.0 %reduce-scatter.9.cloned.1.call-start = ((), (), s32[]{:S(2)}) async-start(), calls=%async_computation.5 | async-start | bytes 10485760 | tf_op jit(solution)/shard_map/reduce_scatter | solution.py:37
  8.7 238.3 %reduce-scatter.7.cloned.1.call-start = ((), (), s32[]{:S(2)}) async-start(), calls=%async_computation.4 | async-start | bytes 23592960 | tf_op jit(solution)/shard_map/reduce_scatter | solution.py:36
  8.7 0.8 copy-start.8
  9.4 262.9 %reduce-scatter.13.cloned.1.call-start = ((), (), s32[]{:S(2)}) async-start(), calls=%async_computation.7 | async-start | bytes 1966080
  11.2 439.4 %all-reduce.3.cloned.1.call-start = ((), (), s32[]{:S(2)}) async-start(), calls=%async_computation.8 | async-start | bytes 15204352 | tf_op jit(solution)/shard_map/psum | solution.py:40
  450.6 4.3 copy-start
  450.6 5.5 %copy-start.1 = (f32[64,3072]{1,0:T(8,128)S(1)}, f32[64,3072]{1,0:T(8,128)}, u32[]{:S(2)}) copy-start(f32[64,3072]{1,0:T(8,128)} %get-tuple-element.18) | copy-start | bytes 2359300
  467.0 13.1 %copy-start.2 = (f32[64,8192]{1,0:T(8,128)S(1)}, f32[64,8192]{1,0:T(8,128)}, u32[]{:S(2)}) copy-start(f32[64,8192]{1,0:T(8,128)} %param.23) | copy-start | bytes 6291460
  467.0 13.1 %copy-start.3 = (f32[64,8192]{1,0:T(8,128)S(1)}, f32[64,8192]{1,0:T(8,128)}, u32[]{:S(2)}) copy-start(f32[64,8192]{1,0:T(8,128)} %param.24) | copy-start | bytes 6291460
  467.0 13.5 %copy-start.4 = (f32[64,8192]{1,0:T(8,128)S(1)}, f32[64,8192]{1,0:T(8,128)}, u32[]{:S(2)}) copy-start(f32[64,8192]{1,0:T(8,128)} %param.25) | copy-start | bytes 6291460
  480.5 4.2 copy-start.5
  480.5 4.2 copy-start.6
  480.5 4.2 copy-start.7
  484.7 2.0 copy-start.9
  484.7 2.0 copy-start.10
  484.7 1.9 copy-start.11
Sparse Core Ops, SparseCore 0:
  10.5 34.7 reduce-scatter.10
  47.8 65.0 reduce-scatter.8
  115.5 131.4 reduce-scatter.6
  249.9 22.3 reduce-scatter.12
  274.7 175.7 all-reduce.2
where the time goes:
time: 494 us
  waiting for transfers between devices  431 us (87%)
  other arithmetic  26.6 us (5%)
  between operations  17.2 us (3%)
  blocking collectives  15.1 us (3%)
    psum x1, waiting for transfers between devices, local_update(): layer_mean = lax.psum(layer_part, 'dp') / dev_count  168 us
    reduce_scatter x1, waiting for transfers between devices, local_update(): lax.psum_scatter(g_layer[0], 'fsdp', scatter_dimension=1, tiled=True)  134 us
    reduce_scatter x1, waiting for transfers between devices, local_update(): lax.psum_scatter(g_down[0], 'fsdp', scatter_dimension=0, tiled=True)  67.7 us
    reduce_scatter x1, waiting for transfers between devices, local_update(): lax.psum_scatter(g_embed[0], 'fsdp', scatter_dimension=0, tiled=True)  34 us
    unnamed x6, waiting for transfers between devices  27.4 us
    convert_element_type x4, other arithmetic, adamw_step(): return (master_new, avg_new, sq_new, master_new.astype(jnp.bfloat16))  19.8 us
  transfers between devices with their start and end apart: 5, of which 5 were waited for; matrix products, arithmetic and copies ran while one was open for 1% of the time, Pallas kernels for 0%

commit v1 on v0

v1 whole, which is shorter than its diff:
```python
import functools

import jax
import jax.numpy as jnp
from jax import lax
from jax.experimental import pallas as pl
from jax.experimental.pallas import tpu as pltpu
from jax.sharding import PartitionSpec as P

ADAM_BETA1 = 0.9
ADAM_BETA2 = 0.95
ADAM_EPS = 1e-8
LEARN_RATE = 4e-4
WEIGHT_DECAY = 0.1
CLIP_EPS = 1e-6
OPT_STEP = 20
BIAS_ONE = 1.0 - ADAM_BETA1 ** OPT_STEP
BIAS_TWO = 1.0 - ADAM_BETA2 ** OPT_STEP

MESH = pl.DeviceIdType.MESH
F32 = jnp.float32

ROWS = 64
WIDTH = 3072
FF = 8192
HALF = FF // 2
NORM = (4, 768)
N_DOWN = 2 * (ROWS // 8)
N_SEVEN = 7 * (ROWS // 8)
N = N_DOWN + N_SEVEN

RING = 8
FETCH = 6
LEAD = 3
LAG = 3


def down_at(k):
    row = pl.multiple_of((k // 2) * 8, 8)
    col = pl.multiple_of((k % 2) * HALF, HALF)
    return row, col


def seven_at(k):
    q = k - N_DOWN
    return q // 8, pl.multiple_of((q % 8) * 8, 8)


def reduce_kernel(g_layer, g_down, g_norm, g_embed, layer_w, layer_m, layer_v, down_w, down_m, down_v,
                  norm_w, norm_m, norm_v, embed_w, embed_m, embed_v,
                  sq_out, g7, gd, gn, w7, m7, v7, wd, md, vd, wn, mn, vn,
                  own_o, par_o, pm7, pmd, x7, xd, y7, yd, own_no, par_no, pmn, xn, yn, acc, sq_all,
                  own_o_sem, own_m_sem, do_send, do_recv, dm_send, dm_recv, x_send, x_recv, y_send, y_recv,
                  st_sem, n_sem, n_send, n_recv, sq_send, sq_recv, credit):
    dp = lax.axis_index("dp")
    f = lax.axis_index("fsdp")
    core = lax.rem(f, 2)
    f_core = f + 1 - 2 * core
    f_x = lax.rem(f + 2, 4)
    f_diag = lax.rem(f_core + 2, 4)
    peer_core = (dp, f_core)
    peer_x = (dp, f_x)
    peer_diag = (dp, f_diag)
    peer_y = (1 - dp, f)

    def remote(src, dst, send, recv, peer):
        return pltpu.make_async_remote_copy(src_ref=src, dst_ref=dst, send_sem=send, recv_sem=recv,
                                            device_id=peer, device_id_type=MESH)

    barrier = pltpu.get_barrier_semaphore()
    for peer in (peer_core, peer_x, peer_diag, peer_y):
        pl.semaphore_signal(barrier, inc=1, device_id=peer, device_id_type=MESH)
    pl.semaphore_wait(barrier, 4)
    acc[...] = jnp.zeros_like(acc)

    def on_chunk(k, on_down, on_seven):
        @pl.when(jnp.logical_and(k >= 0, k < N_DOWN))
        def _():
            on_down()

        @pl.when(jnp.logical_and(k >= N_DOWN, k < N))
        def _():
            on_seven()

    def on_source(k, use):
        def on_down():
            row, col = down_at(k)
            use(lambda q: g_down.at[0, pl.ds(pl.multiple_of(q * ROWS + row, 8), 8), pl.ds(col, HALF)],
                lambda ring, s: ring.at[s],
                lambda seven, down: down.at[pl.ds(row, 8), pl.ds(col, HALF)])

        def on_seven():
            j, row = seven_at(k)

            def view(seven, down):
                return seven.at[j, pl.ds(row, 8), :]

            def ring_view(ring, s):
                return ring.at[s, :, pl.ds(0, WIDTH)]

            @pl.when(j < 6)
            def _():
                use(lambda q: g_layer.at[0, j, pl.ds(pl.multiple_of(q * ROWS + row, 8), 8), :], ring_view, view)

            @pl.when(j == 6)
            def _():
                use(lambda q: g_embed.at[0, pl.ds(pl.multiple_of(q * ROWS + row, 8), 8), :], ring_view, view)

        on_chunk(k, on_down, on_seven)

    def on_view(k, use):
        def on_down():
            row, col = down_at(k)
            use(lambda ring, s: ring.at[s], lambda seven, down: down.at[pl.ds(row, 8), pl.ds(col, HALF)], HALF)

        def on_seven():
            j, row = seven_at(k)
            use(lambda ring, s: ring.at[s, :, pl.ds(0, WIDTH)], lambda seven, down: seven.at[j, pl.ds(row, 8), :],
                WIDTH)

        on_chunk(k, on_down, on_seven)

    def x_copy(k, ring_view, view):
        s = lax.rem(k, RING)
        return remote(ring_view(own_o, s), view(x7, xd), x_send.at[s], x_recv.at[k], peer_x)

    def y_copy(k, view):
        s = lax.rem(k, RING)
        return remote(view(g7, gd), view(y7, yd), y_send.at[s], y_recv.at[k], peer_y)

    def push_other(k, source, ring_view):
        s = lax.rem(k, RING)
        return remote(source(f_diag), ring_view(par_o, s), do_send.at[s], do_recv.at[s], peer_core)

    def push_mine(k, source, view):
        s = lax.rem(k, RING)
        return remote(source(f_core), view(pm7, pmd), dm_send.at[s], dm_recv.at[k], peer_core)

    def fetch(k):
        s = lax.rem(k, RING)

        @pl.when(jnp.logical_and(k >= RING, k < N))
        def _():
            def retire(ring_view, view, width):
                x_copy(k - RING, ring_view, view).wait_send()
                push = remote(ring_view(par_o, s), ring_view(par_o, s), do_send.at[s], do_recv.at[s], peer_core)
                push.wait_send()
                push = remote(view(pm7, pmd), view(pm7, pmd), dm_send.at[s], dm_recv.at[k], peer_core)
                push.wait_send()

            on_view(k - RING, retire)
            pl.semaphore_wait(credit, 1)

        def start(source, ring_view, view):
            push_other(k, source, ring_view).start()
            pltpu.make_async_copy(source(f_x), ring_view(own_o, s), own_o_sem.at[s]).start()
            push_mine(k, source, view).start()
            pltpu.make_async_copy(source(f), view(g7, gd), own_m_sem.at[s]).start()

        on_source(k, start)

    def sum_x(k):
        s = lax.rem(k, RING)

        def use(ring_view, view, width):
            mine = view(g7, gd)
            pltpu.make_async_copy(mine, mine, own_m_sem.at[s]).wait()
            push = remote(view(pm7, pmd), view(pm7, pmd), dm_send.at[s], dm_recv.at[k], peer_core)
            push.wait_recv()
            x_copy(k, ring_view, view).wait_recv()
            mine[...] = (mine[...] + view(pm7, pmd)[...]) + view(x7, xd)[...]

        on_view(k, use)

    def sum_chip(k):
        s = lax.rem(k, RING)

        def use(ring_view, view, width):
            mine = ring_view(own_o, s)
            pltpu.make_async_copy(mine, mine, own_o_sem.at[s]).wait()
            push = remote(ring_view(par_o, s), ring_view(par_o, s), do_send.at[s], do_recv.at[s], peer_core)
            push.wait_recv()
            mine[...] = mine[...] + ring_view(par_o, s)[...]

        on_view(k, use)

    def start_y(k):
        on_view(k, lambda ring_view, view, width: y_copy(k, view).start())

    def start_x(k):
        on_view(k, lambda ring_view, view, width: x_copy(k, ring_view, view).start())

        @pl.when(jnp.logical_and(k >= 0, k < N - RING))
        def _():
            pl.semaphore_signal(credit, inc=1, device_id=peer_core, device_id_type=MESH)

    def state_down(k):
        row, col = down_at(k)
        s = lax.rem(k, RING)
        return [pltpu.make_async_copy(src.at[pl.ds(row, 8), pl.ds(col, HALF)], dst.at[pl.ds(row, 8), pl.ds(col, HALF)],
                                      st_sem.at[i, s])
                for i, (src, dst) in enumerate(((down_w, wd), (down_m, md), (down_v, vd)))]

    def state_layer(k):
        j, row = seven_at(k)
        s = lax.rem(k, RING)
        return [pltpu.make_async_copy(src.at[j, pl.ds(row, 8), :], dst.at[j, pl.ds(row, 8), :], st_sem.at[i, s])
                for i, (src, dst) in enumerate(((layer_w, w7), (layer_m, m7), (layer_v, v7)))]

    def state_embed(k):
        j, row = seven_at(k)
        s = lax.rem(k, RING)
        return [pltpu.make_async_copy(src.at[pl.ds(row, 8), :], dst.at[6, pl.ds(row, 8), :], st_sem.at[i, s])
                for i, (src, dst) in enumerate(((embed_w, w7), (embed_m, m7), (embed_v, v7)))]

    def start_state(k):
        def on_seven():
            j, _ = seven_at(k)

            @pl.when(j < 6)
            def _():
                for copy in state_layer(k):
                    copy.start()

            @pl.when(j == 6)
            def _():
                for copy in state_embed(k):
                    copy.start()

        def on_down():
            for copy in state_down(k):
                copy.start()

        on_chunk(k, on_down, on_seven)

    def sum_y(k):
        s = lax.rem(k, RING)

        def use(ring_view, view, width):
            y_copy(k, view).wait()
            for i, ref in enumerate(((w7, wd), (m7, md), (v7, vd))):
                pltpu.make_async_copy(view(*ref), view(*ref), st_sem.at[i, s]).wait()
            mean = (view(g7, gd)[...] + view(y7, yd)[...]) * 0.125
            view(g7, gd)[...] = mean
            parts = [mean[:, i * 128:(i + 1) * 128] for i in range(width // 128)]
            sums = [p * p for p in parts[:4]]
            for i, p in enumerate(parts[4:]):
                sums[i % 4] = sums[i % 4] + p * p
            acc[...] += (sums[0] + sums[1]) + (sums[2] + sums[3])

        on_view(k, use)

    def norm_source(q):
        return g_norm.at[0, :, pl.ds(pl.multiple_of(q * NORM[1], 128), NORM[1])]

    n_push_other = remote(norm_source(f_diag), par_no, n_send.at[0], n_recv.at[0], peer_core)
    n_push_mine = remote(norm_source(f_core), pmn, n_send.at[1], n_recv.at[1], peer_core)
    n_x = remote(own_no, xn, n_send.at[2], n_recv.at[2], peer_x)
    n_y = remote(gn, yn, n_send.at[3], n_recv.at[3], peer_y)
    n_local = [pltpu.make_async_copy(src, dst, n_sem.at[i]) for i, (src, dst) in enumerate(
        ((norm_source(f_x), own_no), (norm_source(f), gn), (norm_w, wn), (norm_m, mn), (norm_v, vn)))]

    def step(t, _):
        i = t - FETCH
        fetch(i + FETCH)

        @pl.when(i == 0)
        def _():
            n_push_other.start()
            n_push_mine.start()
            for copy in n_local:
                copy.start()

        sum_x(i)
        sum_chip(i + LEAD)
        start_y(i)
        start_x(i + LEAD)
        start_state(i)

        @pl.when(i == 4)
        def _():
            for copy in n_local:
                copy.wait()
            n_push_other.wait()
            n_push_mine.wait()
            own_no[...] = own_no[...] + par_no[...]
            n_x.start()

        @pl.when(i == 10)
        def _():
            n_x.wait()
            gn[...] = (gn[...] + pmn[...]) + xn[...]
            n_y.start()

        @pl.when(i == 16)
        def _():
            n_y.wait()
            mean = (gn[...] + yn[...]) * 0.125
            gn[...] = mean
            square = mean * mean
            total = square[:, 0:128]
            for c in range(1, NORM[1] // 128):
                total = total + square[:, c * 128:(c + 1) * 128]
            acc[0:4, :] += total

        sum_y(i - LAG)
        return 0

    lax.fori_loop(0, FETCH + N + LAG, step, 0)

    sq_all[f] = acc[...]
    copies = [remote(sq_all.at[f], sq_all.at[f], sq_send.at[i], sq_recv.at[i], peer)
              for i, peer in enumerate((peer_core, peer_x, peer_diag))]
    for copy in copies:
        copy.start()

    def drain(k, _):
        s = lax.rem(k, RING)

        def use(ring_view, view, width):
            x_copy(k, ring_view, view).wait_send()
            remote(ring_view(par_o, s), ring_view(par_o, s), do_send.at[s], do_recv.at[s], peer_core).wait_send()
            remote(view(pm7, pmd), view(pm7, pmd), dm_send.at[s], dm_recv.at[k], peer_core).wait_send()

        on_view(k, use)
        return 0

    lax.fori_loop(N - RING, N, drain, 0)
    for copy in copies:
        copy.wait()
    sq_out[...] = (sq_all[0] + sq_all[1]) + (sq_all[2] + sq_all[3])


def update_math(clip, g, w, m, v, decay):
    clipped = clip * g
    avg = ADAM_BETA1 * m + (1.0 - ADAM_BETA1) * clipped
    sq = ADAM_BETA2 * v + (1.0 - ADAM_BETA2) * clipped * clipped
    step_dir = (avg / BIAS_ONE) / (jnp.sqrt(sq / BIAS_TWO) + ADAM_EPS)
    new = w - LEARN_RATE * (step_dir + decay * w)
    return new, avg, sq, new.astype(jnp.bfloat16)


def update_kernel(sq, g7, gd, gn, w7, m7, v7, wd, md, vd, wn, mn, vn,
                  lw, lm, lv, lb, dw, dm, dv, db, nw, nm, nv, nb, ew, em, ev, eb,
                  s7w, s7m, s7v, s7b, sdw, sdm, sdv, sdb, snw, snm, snv, snb, sem7, semd, semn):
    total = jnp.sum(sq[...], keepdims=True)
    clip = jnp.minimum(1.0, 1.0 / (jnp.sqrt(total) + CLIP_EPS))

    def seven_copies(j, row, outs):
        i = row // 16
        return [pltpu.make_async_copy(src.at[j, pl.ds(row, 16), :], dst, sem7.at[a, j, i])
                for a, (src, dst) in enumerate(zip((s7w, s7m, s7v, s7b), outs))]

    def layer_copies(j, row):
        return seven_copies(j, row, [o.at[j, pl.ds(row, 16), :] for o in (lw, lm, lv, lb)])

    def embed_copies(row):
        return seven_copies(6, row, [o.at[pl.ds(row, 16), :] for o in (ew, em, ev, eb)])

    def seven(j, decay, row):
        at = (j, pl.ds(row, 16))
        for c in range(0, WIDTH, 512):
            ix = at + (pl.ds(c, 512),)
            out = update_math(clip, g7[ix], w7[ix], m7[ix], v7[ix], decay)
            for ref, val in zip((s7w, s7m, s7v, s7b), out):
                ref[ix] = val

    def layer_step(t, _):
        j = t // 4
        row = pl.multiple_of((t % 4) * 16, 16)
        seven(j, WEIGHT_DECAY, row)
        for copy in layer_copies(j, row):
            copy.start()
        return 0

    def embed_step(t, _):
        row = pl.multiple_of(t * 16, 16)
        seven(6, 0.0, row)
        for copy in embed_copies(row):
            copy.start()
        return 0

    def down_copies(t):
        row = pl.multiple_of((t // 2) * 16, 16)
        col = pl.multiple_of((t % 2) * HALF, HALF)
        ix = (pl.ds(row, 16), pl.ds(col, HALF))
        return [pltpu.make_async_copy(src.at[ix], dst.at[ix], semd.at[a, t])
                for a, (src, dst) in enumerate(zip((sdw, sdm, sdv, sdb), (dw, dm, dv, db)))]

    def down_step(t, _):
        row = pl.multiple_of((t // 2) * 16, 16)
        col = pl.multiple_of((t % 2) * HALF, HALF)
        for c in range(0, HALF, 512):
            ix = (pl.ds(row, 16), pl.ds(pl.multiple_of(col + c, 512), 512))
            out = update_math(clip, gd[ix], wd[ix], md[ix], vd[ix], WEIGHT_DECAY)
            for ref, val in zip((sdw, sdm, sdv, sdb), out):
                ref[ix] = val
        for copy in down_copies(t):
            copy.start()
        return 0

    lax.fori_loop(0, 8, down_step, 0)
    out = update_math(clip, gn[...], wn[...], mn[...], vn[...], WEIGHT_DECAY)
    for ref, val in zip((snw, snm, snv, snb), out):
        ref[...] = val
    norm_copies = [pltpu.make_async_copy(src, dst, semn.at[a])
                   for a, (src, dst) in enumerate(zip((snw, snm, snv, snb), (nw, nm, nv, nb)))]
    for copy in norm_copies:
        copy.start()
    lax.fori_loop(0, 24, layer_step, 0)
    lax.fori_loop(0, 4, embed_step, 0)

    def layer_wait(t, _):
        for copy in layer_copies(t // 4, pl.multiple_of((t % 4) * 16, 16)):
            copy.wait()
        return 0

    def embed_wait(t, _):
        for copy in embed_copies(pl.multiple_of(t * 16, 16)):
            copy.wait()
        return 0

    def down_wait(t, _):
        for copy in down_copies(t):
            copy.wait()
        return 0

    lax.fori_loop(0, 8, down_wait, 0)
    for copy in norm_copies:
        copy.wait()
    lax.fori_loop(0, 24, layer_wait, 0)
    lax.fori_loop(0, 4, embed_wait, 0)


SEVEN = (7, ROWS, WIDTH)
DOWN = (ROWS, FF)


def local_update(g_layer, g_down, g_norm, g_embed, layer_w, layer_m, layer_v, down_w, down_m, down_v, norm_w, norm_m,
                 norm_v, embed_w, embed_m, embed_v):
    any_spec = pl.BlockSpec(memory_space=pl.ANY)
    vmem_spec = pl.BlockSpec(memory_space=pltpu.VMEM)
    dma = pltpu.SemaphoreType.DMA
    held = [(8, 128)] + [SEVEN, DOWN, NORM] + [SEVEN] * 3 + [DOWN] * 3 + [NORM] * 3
    reduced = pl.pallas_call(
        reduce_kernel,
        out_shape=[pltpu.VMEM(shape, F32) for shape in held],
        in_specs=[any_spec] * 16,
        out_specs=[vmem_spec] * len(held),
        scratch_shapes=[pltpu.VMEM((RING, 8, HALF), F32), pltpu.VMEM((RING, 8, HALF), F32)]
        + [pltpu.VMEM(SEVEN, F32), pltpu.VMEM(DOWN, F32)] * 3
        + [pltpu.VMEM(NORM, F32)] * 5
        + [pltpu.VMEM((8, 128), F32), pltpu.VMEM((4, 8, 128), F32)]
        + [dma((RING,)), dma((RING,)), dma((RING,)), dma((RING,)), dma((RING,)), dma((N,)), dma((RING,)), dma((N,)),
           dma((RING,)), dma((N,)), dma((3, RING)), dma((5,)), dma((4,)), dma((4,)), dma((3,)), dma((3,)),
           pltpu.SemaphoreType.REGULAR],
        compiler_params=pltpu.CompilerParams(collective_id=0, has_side_effects=True,
                                             vmem_limit_bytes=26 * 1024 * 1024),
    )(g_layer, g_down, g_norm, g_embed, layer_w, layer_m, layer_v, down_w, down_m, down_v, norm_w, norm_m, norm_v,
      embed_w, embed_m, embed_v)
    groups = ((6, ROWS, WIDTH), DOWN, NORM, (ROWS, WIDTH))
    out_shape = [jax.ShapeDtypeStruct(s, d) for s in groups for d in (F32, F32, F32, jnp.bfloat16)]
    staged = [pltpu.VMEM(s, d) for s in (SEVEN, DOWN, NORM) for d in (F32, F32, F32, jnp.bfloat16)]
    return pl.pallas_call(
        update_kernel,
        out_shape=out_shape,
        in_specs=[vmem_spec] * len(held),
        out_specs=[any_spec] * 16,
        scratch_shapes=staged + [dma((4, 7, 4)), dma((4, 8)), dma((4,))],
        compiler_params=pltpu.CompilerParams(vmem_limit_bytes=26 * 1024 * 1024),
    )(*[pltpu.with_memory_space_constraint(a, pltpu.VMEM) for a in reduced])


def solution(mesh):
    grad_four = P(("dp", "fsdp"), None, None, None)
    grad_three = P(("dp", "fsdp"), None, None)
    layer_spec = P(None, "fsdp", None)
    down_spec = P("fsdp", None)
    norm_spec = P(None, "fsdp")
    embed_spec = P("fsdp", None)
    in_specs = (grad_four, grad_three, grad_three, grad_three,
                layer_spec, layer_spec, layer_spec, down_spec, down_spec, down_spec,
                norm_spec, norm_spec, norm_spec, embed_spec, embed_spec, embed_spec)
    out_specs = (layer_spec,) * 4 + (down_spec,) * 4 + (norm_spec,) * 4 + (embed_spec,) * 4
    return jax.shard_map(local_update, mesh=mesh, in_specs=in_specs, out_specs=out_specs, check_vma=False)
```

time: 494 us -> 192 us (0.39)
  waiting for transfers between devices: 431 us -> 0 us
  Pallas kernels: 0 us -> 191 us
  other arithmetic: 26.6 us -> 0 us
  between operations: 17.2 us -> 0.66 us
  blocking collectives: 15.1 us -> 0 us
    reduce_scatter x3 -> x0, waiting for transfers between devices: 236 us -> none  [the longest x1 134 us: local_update(): lax.psum_scatter(g_layer[0], 'fsdp', scatter_dimension=1, tiled=True)]
    pallas_call x0 -> x2, Pallas kernels: none -> 191 us  [the longest x1 181 us: local_update(): pl.pallas_call(reduce_kernel, out_shape=[pltpu.VMEM(shape, F32) for shape...]
    psum x1 -> x0, waiting for transfers between devices: 168 us -> none  [local_update(): layer_mean = lax.psum(layer_part, 'dp') / dev_count]
    unnamed x6 -> x0, waiting for transfers between devices: 27.4 us -> none
    convert_element_type x4 -> x0, other arithmetic: 19.8 us -> none  [adamw_step(): return (master_new, avg_new, sq_new, master_new.astype(jnp.bfloat16))]
    psum x2 -> x0, blocking collectives: 15.1 us -> none  [the longest x1 8.34 us: local_update(): norm_mean = lax.psum(norm_part, 'dp') / dev_count]
    reduce_sum x4 -> x0, other arithmetic: 6.85 us -> none  [the longest x1 4.3 us: local_update(): jnp.sum(layer_mean * layer_mean) + jnp.sum(down_mean * down_mean)]
  transfers between devices with their start and end apart: 5 -> 0, of which waited for: 5 -> 0; matrix products, arithmetic and copies ran while one was open for 1% -> 0% of each run, Pallas kernels for 0% -> 0%
where the time goes in v1:
time: 192 us
  Pallas kernels  191 us (99%)
    pallas_call x1, Pallas kernels, local_update(): pl.pallas_call(reduce_kernel, out_shape=[pltpu.VMEM(shape, F32) for shape...  181 us
    pallas_call x1, Pallas kernels, local_update(): pl.pallas_call(update_kernel, out_shape=out_shape, in_specs=[vmem_spec] *...  10.5 us

profile of v1, /device:TPU:0, one launch (start us, length us, event | category | flops | bytes accessed | tf_op | source)
XLA Modules:
  0.0 191.7 jit_solution(13085416146699689529)
XLA Ops:
  0.7 180.6 %shard_map.279 = (f32[8,128]{1,0:T(8,128)S(1)}, f32[7,64,3072]{2,1,0:T(8,128)S(1)}, f32[64,8192]{1,0:T(8,128)S(1)}, f32[4,768]{1,0:T(4,128)S(1)}, f32[7,64,3072]...) custom-call(f32[1,6,256,3072]{3,2,1,0:T(8,128)} %g_layer.1, ...), custom_call_target="tpu_custom_call" | custom-call | tf_op jit(solution)/shard_map/pallas_call | solution.py:445
  181.3 10.5 %shard_map.280 = (f32[6,64,3072]{2,1,0:T(8,128)}, f32[6,64,3072]{2,1,0:T(8,128)}, f32[6,64,3072]{2,1,0:T(8,128)}, bf16[6,64,3072]{2,1,0:T(8,128)(2,1)}, f32[64,8...) custom-call(f32[8,128]{1,0:T(8,128)S(1)} %get-tuple-element.29.sq, ...), custom_call_target="tpu_custom_call" | custom-call | tf_op jit(solution)/shard_map/pallas_call | solution.py:464

commit v2 on v1

--- a/solution.py
+++ b/solution.py
@@ -1,4 +1,4 @@
-import functools
+import math
 
 import jax
 import jax.numpy as jnp
@@ -16,6 +16,8 @@
 OPT_STEP = 20
 BIAS_ONE = 1.0 - ADAM_BETA1 ** OPT_STEP
 BIAS_TWO = 1.0 - ADAM_BETA2 ** OPT_STEP
+ROOT_TWO = math.sqrt(BIAS_TWO)
+SMALLEST = 1.1754944e-38
 
 MESH = pl.DeviceIdType.MESH
 F32 = jnp.float32
@@ -23,35 +25,48 @@
 ROWS = 64
 WIDTH = 3072
 FF = 8192
-HALF = FF // 2
+PIECE = 2048
 NORM = (4, 768)
-N_DOWN = 2 * (ROWS // 8)
-N_SEVEN = 7 * (ROWS // 8)
-N = N_DOWN + N_SEVEN
-
-RING = 8
-FETCH = 6
-LEAD = 3
-LAG = 3
+SEVEN = (7, ROWS, WIDTH)
+DOWN = (ROWS, FF)
+
+FIRST = 16
+N_SEVEN = 7 * (ROWS // 8) - FIRST // 8
+N_DOWN = (FF // PIECE) * (ROWS // 8)
+N = N_SEVEN + N_DOWN
+
+RING = 12
+FETCH = 8
+LEAD = 4
+LAG = 4
+
+
+def seven_at(k):
+    return k // 8, pl.multiple_of((k % 8) * 8, 8)
 
 
 def down_at(k):
-    row = pl.multiple_of((k // 2) * 8, 8)
-    col = pl.multiple_of((k % 2) * HALF, HALF)
+    q = k - N_SEVEN
+    row = pl.multiple_of((q // 4) * 8, 8)
+    col = pl.multiple_of((q % 4) * PIECE, PIECE)
     return row, col
 
 
-def seven_at(k):
-    q = k - N_DOWN
-    return q // 8, pl.multiple_of((q % 8) * 8, 8)
+def squares(mean, width):
+    parts = [mean[:, i * 128:(i + 1) * 128] for i in range(width // 128)]
+    sums = [p * p for p in parts[:4]]
+    for i, p in enumerate(parts[4:]):
+        sums[i % 4] = sums[i % 4] + p * p
+    return (sums[0] + sums[1]) + (sums[2] + sums[3])
 
 
 def reduce_kernel(g_layer, g_down, g_norm, g_embed, layer_w, layer_m, layer_v, down_w, down_m, down_v,
                   norm_w, norm_m, norm_v, embed_w, embed_m, embed_v,
                   sq_out, g7, gd, gn, w7, m7, v7, wd, md, vd, wn, mn, vn,
-                  own_o, par_o, pm7, pmd, x7, xd, y7, yd, own_no, par_no, pmn, xn, yn, acc, sq_all,
+                  own_o, par_o, pm7, pmd, x7, xd, y7, yd, own_no, par_no, pmn, xn, yn, acc, sq_all, sq_first,
+                  fo_own, fo_par, fm_own, fm_par, f_y, f_x_in, f_out, f_in,
                   own_o_sem, own_m_sem, do_send, do_recv, dm_send, dm_recv, x_send, x_recv, y_send, y_recv,
-                  st_sem, n_sem, n_send, n_recv, sq_send, sq_recv, credit):
+                  st_sem, n_sem, n_send, n_recv, sq_send, sq_recv, sqf_send, sqf_recv, f_sem, f_send, f_recv, credit):
     dp = lax.axis_index("dp")
     f = lax.axis_index("fsdp")
     core = lax.rem(f, 2)
@@ -62,32 +77,33 @@
     peer_x = (dp, f_x)
     peer_diag = (dp, f_diag)
     peer_y = (1 - dp, f)
+    peers = (peer_core, peer_x, peer_diag, peer_y, (1 - dp, f_core), (1 - dp, f_x), (1 - dp, f_diag))
 
     def remote(src, dst, send, recv, peer):
         return pltpu.make_async_remote_copy(src_ref=src, dst_ref=dst, send_sem=send, recv_sem=recv,
                                             device_id=peer, device_id_type=MESH)
 
     barrier = pltpu.get_barrier_semaphore()
-    for peer in (peer_core, peer_x, peer_diag, peer_y):
+    for peer in peers:
         pl.semaphore_signal(barrier, inc=1, device_id=peer, device_id_type=MESH)
-    pl.semaphore_wait(barrier, 4)
+    pl.semaphore_wait(barrier, len(peers))
     acc[...] = jnp.zeros_like(acc)
 
     def on_chunk(k, on_down, on_seven):
-        @pl.when(jnp.logical_and(k >= 0, k < N_DOWN))
+        @pl.when(jnp.logical_and(k >= 0, k < N_SEVEN))
+        def _():
+            on_seven()
+
+        @pl.when(jnp.logical_and(k >= N_SEVEN, k < N))
         def _():
             on_down()
-
-        @pl.when(jnp.logical_and(k >= N_DOWN, k < N))
-        def _():
-            on_seven()
 
     def on_source(k, use):
         def on_down():
             row, col = down_at(k)
-            use(lambda q: g_down.at[0, pl.ds(pl.multiple_of(q * ROWS + row, 8), 8), pl.ds(col, HALF)],
-                lambda ring, s: ring.at[s],
-                lambda seven, down: down.at[pl.ds(row, 8), pl.ds(col, HALF)])
+            use(lambda q: g_down.at[0, pl.ds(pl.multiple_of(q * ROWS + row, 8), 8), pl.ds(col, PIECE)],
+                lambda ring, s: ring.at[s, :, pl.ds(0, PIECE)],
+                lambda seven, down: down.at[pl.ds(row, 8), pl.ds(col, PIECE)])
 
         def on_seven():
             j, row = seven_at(k)
@@ -96,7 +112,7 @@
                 return seven.at[j, pl.ds(row, 8), :]
 
             def ring_view(ring, s):
-                return ring.at[s, :, pl.ds(0, WIDTH)]
+                return ring.at[s]
 
             @pl.when(j < 6)
             def _():
@@ -111,12 +127,12 @@
     def on_view(k, use):
         def on_down():
             row, col = down_at(k)
-            use(lambda ring, s: ring.at[s], lambda seven, down: down.at[pl.ds(row, 8), pl.ds(col, HALF)], HALF)
+            use(lambda ring, s: ring.at[s, :, pl.ds(0, PIECE)],
+                lambda seven, down: down.at[pl.ds(row, 8), pl.ds(col, PIECE)], PIECE)
 
         def on_seven():
             j, row = seven_at(k)
-            use(lambda ring, s: ring.at[s, :, pl.ds(0, WIDTH)], lambda seven, down: seven.at[j, pl.ds(row, 8), :],
-                WIDTH)
+            use(lambda ring, s: ring.at[s], lambda seven, down: seven.at[j, pl.ds(row, 8), :], WIDTH)
 
         on_chunk(k, on_down, on_seven)
 
@@ -197,7 +213,7 @@
     def state_down(k):
         row, col = down_at(k)
         s = lax.rem(k, RING)
-        return [pltpu.make_async_copy(src.at[pl.ds(row, 8), pl.ds(col, HALF)], dst.at[pl.ds(row, 8), pl.ds(col, HALF)],
+        return [pltpu.make_async_copy(src.at[pl.ds(row, 8), pl.ds(col, PIECE)], dst.at[pl.ds(row, 8), pl.ds(col, PIECE)],
                                       st_sem.at[i, s])
                 for i, (src, dst) in enumerate(((down_w, wd), (down_m, md), (down_v, vd)))]
 
@@ -242,13 +258,31 @@
                 pltpu.make_async_copy(view(*ref), view(*ref), st_sem.at[i, s]).wait()
             mean = (view(g7, gd)[...] + view(y7, yd)[...]) * 0.125
             view(g7, gd)[...] = mean
-            parts = [mean[:, i * 128:(i + 1) * 128] for i in range(width // 128)]
-            sums = [p * p for p in parts[:4]]
-            for i, p in enumerate(parts[4:]):
-                sums[i % 4] = sums[i % 4] + p * p
-            acc[...] += (sums[0] + sums[1]) + (sums[2] + sums[3])
+            acc[...] += squares(mean, width)
 
         on_view(k, use)
+
+    def embed_rows(q):
+        return g_embed.at[0, pl.ds(pl.multiple_of(q * ROWS + (ROWS - FIRST), 8), FIRST), :]
+
+    f_push = [remote(embed_rows(f_diag), fo_par, f_send.at[0], f_recv.at[0], peer_core),
+              remote(embed_rows(f_core), fm_par, f_send.at[1], f_recv.at[1], peer_core)]
+    f_local = [pltpu.make_async_copy(src, dst, f_sem.at[i]) for i, (src, dst) in enumerate(
+        ((embed_rows(f_x), fo_own), (embed_rows(f), fm_own)))]
+    last = pl.ds(ROWS - FIRST, FIRST)
+    f_state = [pltpu.make_async_copy(src.at[last, :], dst.at[6, last, :], f_sem.at[2 + i])
+               for i, (src, dst) in enumerate(((embed_w, w7), (embed_m, m7), (embed_v, v7)))]
+    keep = pl.ds(pl.multiple_of(dp * 8, 8), 8)
+    give = pl.ds(pl.multiple_of((1 - dp) * 8, 8), 8)
+    keep_out = pl.ds(pl.multiple_of(ROWS - FIRST + dp * 8, 8), 8)
+    give_out = pl.ds(pl.multiple_of(ROWS - FIRST + (1 - dp) * 8, 8), 8)
+    f_scatter = [remote(fo_own.at[give, :], f_y.at[0], f_send.at[2], f_recv.at[2], peer_y),
+                 remote(fm_own.at[give, :], f_y.at[1], f_send.at[3], f_recv.at[3], peer_y)]
+    f_cross = remote(fo_own.at[keep, :], f_x_in, f_send.at[4], f_recv.at[4], peer_x)
+    f_gather = remote(f_out, f_in, f_send.at[5], f_recv.at[5], peer_y)
+    me = dp * 4 + f
+    sqf_copies = [remote(sq_first.at[me], sq_first.at[me], sqf_send.at[i], sqf_recv.at[i], peer)
+                  for i, peer in enumerate(peers)]
 
     def norm_source(q):
         return g_norm.at[0, :, pl.ds(pl.multiple_of(q * NORM[1], 128), NORM[1])]
@@ -264,7 +298,14 @@
         i = t - FETCH
         fetch(i + FETCH)
 
-        @pl.when(i == 0)
+        @pl.when(i == -FETCH)
+        def _():
+            for copy in f_push:
+                copy.start()
+            for copy in f_local:
+                copy.start()
+
+        @pl.when(i == -LEAD - 1)
         def _():
             n_push_other.start()
             n_push_mine.start()
@@ -277,7 +318,20 @@
         start_x(i + LEAD)
         start_state(i)
 
-        @pl.when(i == 4)
+        @pl.when(i == 1 - LEAD)
+        def _():
+            for copy in f_local:
+                copy.wait()
+            for copy in f_push:
+                copy.wait()
+            fo_own[...] = fo_own[...] + fo_par[...]
+            fm_own[...] = fm_own[...] + fm_par[...]
+            for copy in f_scatter:
+                copy.start()
+            for copy in f_state:
+                copy.start()
+
+        @pl.when(i == 2)
         def _():
             for copy in n_local:
                 copy.wait()
@@ -291,8 +345,12 @@
             n_x.wait()
             gn[...] = (gn[...] + pmn[...]) + xn[...]
             n_y.start()
-
-        @pl.when(i == 16)
+            for copy in f_scatter:
+                copy.wait()
+            fo_own[keep, :] = fo_own[keep, :] + f_y[0]
+            fm_own[keep, :] = fm_own[keep, :] + f_y[1]
+
+        @pl.when(i == 20)
         def _():
             n_y.wait()
             mean = (gn[...] + yn[...]) * 0.125
@@ -303,6 +361,21 @@
                 total = total + square[:, c * 128:(c + 1) * 128]
             acc[0:4, :] += total
 
+        @pl.when(i == N - LEAD)
+        def _():
+            f_cross.start()
+
+        @pl.when(i == N + LAG - 2)
+        def _():
+            f_cross.wait()
+            mean = (fm_own[keep, :] + f_x_in[...]) * 0.125
+            f_out[...] = mean
+            g7[6, keep_out, :] = mean
+            sq_first[me] = squares(mean, WIDTH)
+            f_gather.start()
+            for copy in sqf_copies:
+                copy.start()
+
         sum_y(i - LAG)
         return 0
 
@@ -326,17 +399,27 @@
         return 0
 
     lax.fori_loop(N - RING, N, drain, 0)
+    for copy in f_state:
+        copy.wait()
+    f_gather.wait()
+    g7[6, give_out, :] = f_in[...]
+    for copy in sqf_copies:
+        copy.wait()
+    total = sq_first[0]
+    for i in range(1, 8):
+        total = total + sq_first[i]
     for copy in copies:
         copy.wait()
-    sq_out[...] = (sq_all[0] + sq_all[1]) + (sq_all[2] + sq_all[3])
-
-
-def update_math(clip, g, w, m, v, decay):
-    clipped = clip * g
-    avg = ADAM_BETA1 * m + (1.0 - ADAM_BETA1) * clipped
-    sq = ADAM_BETA2 * v + (1.0 - ADAM_BETA2) * clipped * clipped
-    step_dir = (avg / BIAS_ONE) / (jnp.sqrt(sq / BIAS_TWO) + ADAM_EPS)
-    new = w - LEARN_RATE * (step_dir + decay * w)
+    sq_out[...] = ((sq_all[0] + sq_all[1]) + (sq_all[2] + sq_all[3])) + total
+
+
+def update_math(avg_scale, sq_scale, g, w, m, v, decay):
+    avg = ADAM_BETA1 * m + avg_scale * g
+    root = sq_scale * g
+    sq = ADAM_BETA2 * v + root * root
+    dev = sq * lax.rsqrt(jnp.maximum(sq, SMALLEST))
+    step_dir = avg / (dev + ADAM_EPS * ROOT_TWO)
+    new = (1.0 - LEARN_RATE * decay) * w - (LEARN_RATE * ROOT_TWO / BIAS_ONE) * step_dir
     return new, avg, sq, new.astype(jnp.bfloat16)
 
 
@@ -345,6 +428,7 @@
                   s7w, s7m, s7v, s7b, sdw, sdm, sdv, sdb, snw, snm, snv, snb, sem7, semd, semn):
     total = jnp.sum(sq[...], keepdims=True)
     clip = jnp.minimum(1.0, 1.0 / (jnp.sqrt(total) + CLIP_EPS))
+    scales = ((1.0 - ADAM_BETA1) * clip, math.sqrt(1.0 - ADAM_BETA2) * clip)
 
     def seven_copies(j, row, outs):
         i = row // 16
@@ -361,7 +445,7 @@
         at = (j, pl.ds(row, 16))
         for c in range(0, WIDTH, 512):
             ix = at + (pl.ds(c, 512),)
-            out = update_math(clip, g7[ix], w7[ix], m7[ix], v7[ix], decay)
+            out = update_math(*scales, g7[ix], w7[ix], m7[ix], v7[ix], decay)
             for ref, val in zip((s7w, s7m, s7v, s7b), out):
                 ref[ix] = val
 
@@ -382,17 +466,17 @@
 
     def down_copies(t):
         row = pl.multiple_of((t // 2) * 16, 16)
-        col = pl.multiple_of((t % 2) * HALF, HALF)
-        ix = (pl.ds(row, 16), pl.ds(col, HALF))
+        col = pl.multiple_of((t % 2) * (FF // 2), FF // 2)
+        ix = (pl.ds(row, 16), pl.ds(col, FF // 2))
         return [pltpu.make_async_copy(src.at[ix], dst.at[ix], semd.at[a, t])
                 for a, (src, dst) in enumerate(zip((sdw, sdm, sdv, sdb), (dw, dm, dv, db)))]
 
     def down_step(t, _):
         row = pl.multiple_of((t // 2) * 16, 16)
-        col = pl.multiple_of((t % 2) * HALF, HALF)
-        for c in range(0, HALF, 512):
+        col = pl.multiple_of((t % 2) * (FF // 2), FF // 2)
+        for c in range(0, FF // 2, 512):
             ix = (pl.ds(row, 16), pl.ds(pl.multiple_of(col + c, 512), 512))
-            out = update_math(clip, gd[ix], wd[ix], md[ix], vd[ix], WEIGHT_DECAY)
+            out = update_math(*scales, gd[ix], wd[ix], md[ix], vd[ix], WEIGHT_DECAY)
             for ref, val in zip((sdw, sdm, sdv, sdb), out):
                 ref[ix] = val
         for copy in down_copies(t):
@@ -400,7 +484,7 @@
         return 0
 
     lax.fori_loop(0, 8, down_step, 0)
-    out = update_math(clip, gn[...], wn[...], mn[...], vn[...], WEIGHT_DECAY)
+    out = update_math(*scales, gn[...], wn[...], mn[...], vn[...], WEIGHT_DECAY)
     for ref, val in zip((snw, snm, snv, snb), out):
         ref[...] = val
     norm_copies = [pltpu.make_async_copy(src, dst, semn.at[a])
@@ -430,10 +514,6 @@
         copy.wait()
     lax.fori_loop(0, 24, layer_wait, 0)
     lax.fori_loop(0, 4, embed_wait, 0)
-
-
-SEVEN = (7, ROWS, WIDTH)
-DOWN = (ROWS, FF)
 
 
 def local_update(g_layer, g_down, g_norm, g_embed, layer_w, layer_m, layer_v, down_w, down_m, down_v, norm_w, norm_m,
@@ -447,12 +527,15 @@
         out_shape=[pltpu.VMEM(shape, F32) for shape in held],
         in_specs=[any_spec] * 16,
         out_specs=[vmem_spec] * len(held),
-        scratch_shapes=[pltpu.VMEM((RING, 8, HALF), F32), pltpu.VMEM((RING, 8, HALF), F32)]
+        scratch_shapes=[pltpu.VMEM((RING, 8, WIDTH), F32), pltpu.VMEM((RING, 8, WIDTH), F32)]
         + [pltpu.VMEM(SEVEN, F32), pltpu.VMEM(DOWN, F32)] * 3
         + [pltpu.VMEM(NORM, F32)] * 5
-        + [pltpu.VMEM((8, 128), F32), pltpu.VMEM((4, 8, 128), F32)]
+        + [pltpu.VMEM((8, 128), F32), pltpu.VMEM((4, 8, 128), F32), pltpu.VMEM((8, 8, 128), F32)]
+        + [pltpu.VMEM((FIRST, WIDTH), F32)] * 4
+        + [pltpu.VMEM((2, 8, WIDTH), F32)] + [pltpu.VMEM((8, WIDTH), F32)] * 3
         + [dma((RING,)), dma((RING,)), dma((RING,)), dma((RING,)), dma((RING,)), dma((N,)), dma((RING,)), dma((N,)),
            dma((RING,)), dma((N,)), dma((3, RING)), dma((5,)), dma((4,)), dma((4,)), dma((3,)), dma((3,)),
+           dma((7,)), dma((7,)), dma((5,)), dma((6,)), dma((6,)),
            pltpu.SemaphoreType.REGULAR],
         compiler_params=pltpu.CompilerParams(collective_id=0, has_side_effects=True,
                                              vmem_limit_bytes=26 * 1024 * 1024),

time: 192 us -> 189 us (0.984)
  Pallas kernels: 191 us -> 188 us
    pallas_call x1, Pallas kernels: 181 us -> 178 us  [local_update(): pl.pallas_call(reduce_kernel, out_shape=[pltpu.VMEM(shape, F32) for shape...]
where the time goes in v2:
time: 189 us
  Pallas kernels  188 us (99%)
    pallas_call x1, Pallas kernels, local_update(): pl.pallas_call(reduce_kernel, out_shape=[pltpu.VMEM(shape, F32) for shape...  178 us
    pallas_call x1, Pallas kernels, local_update(): pl.pallas_call(update_kernel, out_shape=out_shape, in_specs=[vmem_spec] *...  10.4 us

profile of v2, /device:TPU:0, one launch (start us, length us, event | category | flops | bytes accessed | tf_op | source)
XLA Modules:
  0.0 188.9 jit_solution(619344640350258913)
XLA Ops:
  0.7 177.9 %shard_map.279 = (f32[8,128]{1,0:T(8,128)S(1)}, f32[7,64,3072]{2,1,0:T(8,128)S(1)}, f32[64,8192]{1,0:T(8,128)S(1)}, f32[4,768]{1,0:T(4,128)S(1)}, f32[7,64,3072]...) custom-call(f32[1,6,256,3072]{3,2,1,0:T(8,128)} %g_layer.1, ...), custom_call_target="tpu_custom_call" | custom-call | tf_op jit(solution)/shard_map/pallas_call | solution.py:525
  178.6 10.4 %shard_map.280 = (f32[6,64,3072]{2,1,0:T(8,128)}, f32[6,64,3072]{2,1,0:T(8,128)}, f32[6,64,3072]{2,1,0:T(8,128)}, bf16[6,64,3072]{2,1,0:T(8,128)(2,1)}, f32[64,8...) custom-call(f32[8,128]{1,0:T(8,128)S(1)} %get-tuple-element.29.sq, ...), custom_call_target="tpu_custom_call" | custom-call | tf_op jit(solution)/shard_map/pallas_call | solution.py:547

commit v3 on v2

v3 whole, which is shorter than its diff:
```python
import math

import jax
import jax.numpy as jnp
from jax import lax
from jax.experimental import pallas as pl
from jax.experimental.pallas import tpu as pltpu
from jax.sharding import PartitionSpec as P

ADAM_BETA1 = 0.9
ADAM_BETA2 = 0.95
ADAM_EPS = 1e-8
LEARN_RATE = 4e-4
WEIGHT_DECAY = 0.1
CLIP_EPS = 1e-6
OPT_STEP = 20
BIAS_ONE = 1.0 - ADAM_BETA1 ** OPT_STEP
BIAS_TWO = 1.0 - ADAM_BETA2 ** OPT_STEP
ROOT_TWO = math.sqrt(BIAS_TWO)
SMALLEST = 1.1754944e-38

MESH = pl.DeviceIdType.MESH
F32 = jnp.float32

ROWS = 64
WIDTH = 3072
FF = 8192
PIECE = 2048
NORM = (4, 768)
SEVEN = (7, ROWS, WIDTH)
DOWN = (ROWS, FF)

FIRST = 16
N_EMBED = (ROWS - FIRST) // 8
N_LAYER = N_EMBED + 6 * (ROWS // 16)
N_WIDE = N_LAYER + (FF // PIECE) * (ROWS // 16 - 1)
N = N_WIDE + (FF // PIECE) * 2

RING = 7
FETCH = 5
LEAD = 3
LAG = 3


class Chunk:
    def __init__(self, kind, k):
        self.kind = kind
        if kind == "embed":
            self.rows, self.width = 8, WIDTH
            self.row = pl.multiple_of(k * 8, 8)
        elif kind == "layer":
            q = k - N_EMBED
            self.rows, self.width = 16, WIDTH
            self.j = q // 4
            self.row = pl.multiple_of((q % 4) * 16, 16)
        else:
            wide = kind == "wide"
            q = k - (N_LAYER if wide else N_WIDE)
            self.rows, self.width = (16, PIECE) if wide else (8, PIECE)
            start = 0 if wide else ROWS - 16
            self.row = pl.multiple_of(start + (q // 4) * self.rows, 8)
            self.cols = pl.ds(pl.multiple_of((q % 4) * PIECE, PIECE), PIECE)

    def source(self, grads, q):
        g_layer, g_down, g_embed = grads
        rows = pl.ds(pl.multiple_of(q * ROWS + self.row, 8), self.rows)
        if self.kind == "embed":
            return g_embed.at[0, rows, :]
        if self.kind == "layer":
            return g_layer.at[0, self.j, rows, :]
        return g_down.at[0, rows, self.cols]

    def state(self, layer, down, embed):
        rows = pl.ds(self.row, self.rows)
        if self.kind == "embed":
            return embed.at[rows, :]
        if self.kind == "layer":
            return layer.at[self.j, rows, :]
        return down.at[rows, self.cols]

    def held(self, seven, down):
        rows = pl.ds(self.row, self.rows)
        if self.kind == "embed":
            return seven.at[6, rows, :]
        if self.kind == "layer":
            return seven.at[self.j, rows, :]
        return down.at[rows, self.cols]

    def ring(self, ring, s):
        return ring.at[s, pl.ds(0, self.rows), pl.ds(0, self.width)]


def on_chunk(k, use):
    bounds = (0, N_EMBED, N_LAYER, N_WIDE, N)
    for i, kind in enumerate(("embed", "layer", "wide", "down")):
        @pl.when(jnp.logical_and(k >= bounds[i], k < bounds[i + 1]))
        def _():
            use(Chunk(kind, k))


def squares(mean, width):
    parts = [mean[r:r + 8, i * 128:(i + 1) * 128] for r in range(0, mean.shape[0], 8) for i in range(width // 128)]
    sums = [p * p for p in parts[:4]]
    for i, p in enumerate(parts[4:]):
        sums[i % 4] = sums[i % 4] + p * p
    return (sums[0] + sums[1]) + (sums[2] + sums[3])


def reduce_kernel(g_layer, g_down, g_norm, g_embed, layer_w, layer_m, layer_v, down_w, down_m, down_v,
                  norm_w, norm_m, norm_v, embed_w, embed_m, embed_v,
                  sq_out, g7, gd, gn, w7, m7, v7, wd, md, vd, wn, mn, vn,
                  own_o, par_o, pm7, pmd, x7, xd, y7, yd, own_no, par_no, pmn, xn, yn, acc, sq_all, sq_first,
                  pre, fo_own, fo_par, fm_own, fm_par, f_y, f_x_in, f_out, f_in,
                  own_o_sem, own_m_sem, do_send, do_recv, dm_send, dm_recv, x_send, x_recv, y_send, y_recv,
                  st_sem, n_sem, n_send, n_recv, sq_send, sq_recv, sqf_send, sqf_recv, f_sem, f_send, f_recv, pre_sem, credit):
    dp = lax.axis_index("dp")
    f = lax.axis_index("fsdp")
    core = lax.rem(f, 2)
    f_core = f + 1 - 2 * core
    f_x = lax.rem(f + 2, 4)
    f_diag = lax.rem(f_core + 2, 4)
    peer_core = (dp, f_core)
    peer_x = (dp, f_x)
    peer_diag = (dp, f_diag)
    peer_y = (1 - dp, f)
    peers = (peer_core, peer_x, peer_diag, peer_y, (1 - dp, f_core), (1 - dp, f_x), (1 - dp, f_diag))

    def remote(src, dst, send, recv, peer):
        return pltpu.make_async_remote_copy(src_ref=src, dst_ref=dst, send_sem=send, recv_sem=recv,
                                            device_id=peer, device_id_type=MESH)

    grads = (g_layer, g_down, g_embed)

    def x_copy(k, chunk):
        s = lax.rem(k, RING)
        return remote(chunk.ring(own_o, s), chunk.held(x7, xd), x_send.at[s], x_recv.at[k], peer_x)

    def y_copy(k, chunk):
        s = lax.rem(k, RING)
        return remote(chunk.held(g7, gd), chunk.held(y7, yd), y_send.at[s], y_recv.at[k], peer_y)

    def push_other(k, chunk, source):
        s = lax.rem(k, RING)
        return remote(source, chunk.ring(par_o, s), do_send.at[s], do_recv.at[s], peer_core)

    def push_mine(k, chunk, source):
        s = lax.rem(k, RING)
        return remote(source, chunk.held(pm7, pmd), dm_send.at[s], dm_recv.at[k], peer_core)

    def own_loads(k, chunk):
        s = lax.rem(k, RING)
        return [pltpu.make_async_copy(chunk.source(grads, f_x), chunk.ring(own_o, s), own_o_sem.at[s]),
                pltpu.make_async_copy(chunk.source(grads, f), chunk.held(g7, gd), own_m_sem.at[s])]

    def retire(k, chunk):
        s = lax.rem(k, RING)
        x_copy(k, chunk).wait_send()
        push_other(k, chunk, chunk.ring(par_o, s)).wait_send()
        push_mine(k, chunk, chunk.held(pm7, pmd)).wait_send()

    def fetch(k):
        @pl.when(jnp.logical_and(k >= RING, k < N))
        def _():
            on_chunk(k - RING, lambda chunk: retire(k - RING, chunk))
            pl.semaphore_wait(credit, 1)

        def start(chunk):
            push_other(k, chunk, chunk.source(grads, f_diag)).start()
            for copy in own_loads(k, chunk):
                copy.start()
            push_mine(k, chunk, chunk.source(grads, f_core)).start()

        on_chunk(k, start)

    def sum_x(k):
        s = lax.rem(k, RING)

        def use(chunk):
            mine = chunk.held(g7, gd)
            theirs = chunk.held(pm7, pmd)
            pltpu.make_async_copy(mine, mine, own_m_sem.at[s]).wait()
            push_mine(k, chunk, theirs).wait_recv()
            x_copy(k, chunk).wait_recv()
            mine[...] = (mine[...] + theirs[...]) + chunk.held(x7, xd)[...]

        on_chunk(k, use)

    def sum_chip(k):
        s = lax.rem(k, RING)

        def use(chunk):
            mine = chunk.ring(own_o, s)
            theirs = chunk.ring(par_o, s)
            pltpu.make_async_copy(mine, mine, own_o_sem.at[s]).wait()
            push_other(k, chunk, theirs).wait_recv()
            mine[...] = mine[...] + theirs[...]

        on_chunk(k, use)

    def start_x(k):
        on_chunk(k, lambda chunk: x_copy(k, chunk).start())

        @pl.when(jnp.logical_and(k >= 0, k < N - RING))
        def _():
            pl.semaphore_signal(credit, inc=1, device_id=peer_core, device_id_type=MESH)

    def start_y(k):
        s = lax.rem(k, RING)

        def use(chunk):
            y_copy(k, chunk).start()
            for i, (src, dst) in enumerate((((layer_w, down_w, embed_w), (w7, wd)), ((layer_m, down_m, embed_m), (m7, md)),
                                            ((layer_v, down_v, embed_v), (v7, vd)))):
                pltpu.make_async_copy(chunk.state(*src), chunk.held(*dst), st_sem.at[i, s]).start()

        on_chunk(k, use)

    def sum_y(k):
        s = lax.rem(k, RING)

        def use(chunk):
            y_copy(k, chunk).wait()
            for i, pair in enumerate(((w7, wd), (m7, md), (v7, vd))):
                ref = chunk.held(*pair)
                pltpu.make_async_copy(ref, ref, st_sem.at[i, s]).wait()
            mine = chunk.held(g7, gd)
            mean = (mine[...] + chunk.held(y7, yd)[...]) * 0.125
            mine[...] = mean
            acc[...] += squares(mean, chunk.width)

        on_chunk(k, use)

    def embed_rows(q):
        return g_embed.at[0, pl.ds(pl.multiple_of(q * ROWS + (ROWS - FIRST), 8), FIRST), :]

    f_give = [pltpu.make_async_copy(embed_rows(q), own_o.at[RING - 2 + i], f_sem.at[5 + i])
              for i, q in enumerate((f_diag, f_core))]
    f_push = [remote(own_o.at[RING - 2], fo_par, f_send.at[0], f_recv.at[0], peer_core),
              remote(own_o.at[RING - 1], fm_par, f_send.at[1], f_recv.at[1], peer_core)]
    f_local = [pltpu.make_async_copy(src, dst, f_sem.at[i]) for i, (src, dst) in enumerate(
        ((embed_rows(f_x), fo_own), (embed_rows(f), fm_own)))]
    last = pl.ds(ROWS - FIRST, FIRST)
    f_state = [pltpu.make_async_copy(src.at[last, :], dst.at[6, last, :], f_sem.at[2 + i])
               for i, (src, dst) in enumerate(((embed_w, w7), (embed_m, m7), (embed_v, v7)))]
    keep = pl.ds(pl.multiple_of(dp * 8, 8), 8)
    give = pl.ds(pl.multiple_of((1 - dp) * 8, 8), 8)
    keep_out = pl.ds(pl.multiple_of(ROWS - FIRST + dp * 8, 8), 8)
    give_out = pl.ds(pl.multiple_of(ROWS - FIRST + (1 - dp) * 8, 8), 8)
    f_scatter = [remote(fo_own.at[give, :], f_y.at[0], f_send.at[2], f_recv.at[2], peer_y),
                 remote(fm_own.at[give, :], f_y.at[1], f_send.at[3], f_recv.at[3], peer_y)]
    f_cross = remote(fo_own.at[keep, :], f_x_in, f_send.at[4], f_recv.at[4], peer_x)
    f_gather = remote(f_out, f_in, f_send.at[5], f_recv.at[5], peer_y)
    me = dp * 4 + f
    sqf_copies = [remote(sq_first.at[me], sq_first.at[me], sqf_send.at[i], sqf_recv.at[i], peer)
                  for i, peer in enumerate(peers)]

    def norm_source(q):
        return g_norm.at[0, :, pl.ds(pl.multiple_of(q * NORM[1], 128), NORM[1])]

    n_push_other = remote(norm_source(f_diag), par_no, n_send.at[0], n_recv.at[0], peer_core)
    n_push_mine = remote(norm_source(f_core), pmn, n_send.at[1], n_recv.at[1], peer_core)
    n_x = remote(own_no, xn, n_send.at[2], n_recv.at[2], peer_x)
    n_y = remote(gn, yn, n_send.at[3], n_recv.at[3], peer_y)
    n_local = [pltpu.make_async_copy(src, dst, n_sem.at[i]) for i, (src, dst) in enumerate(
        ((norm_source(f_x), own_no), (norm_source(f), gn), (norm_w, wn), (norm_m, mn), (norm_v, vn)))]

    zero = Chunk("embed", 0)
    ahead = pltpu.make_async_copy(zero.source(grads, f_diag), pre, pre_sem)
    ahead.start()
    for copy in own_loads(0, zero):
        copy.start()
    for copy in f_give + f_local:
        copy.start()
    acc[...] = jnp.zeros_like(acc)

    barrier = pltpu.get_barrier_semaphore()
    for peer in peers:
        pl.semaphore_signal(barrier, inc=1, device_id=peer, device_id_type=MESH)
    ahead.wait()
    pl.semaphore_wait(barrier, len(peers))
    push_other(0, zero, pre).start()
    for copy, push in zip(f_give, f_push):
        copy.wait()
        push.start()
    push_mine(0, zero, zero.source(grads, f_core)).start()

    def step(t, _):
        i = t - FETCH
        fetch(i + FETCH)

        @pl.when(i == 0)
        def _():
            n_push_other.start()
            n_push_mine.start()
            for copy in n_local:
                copy.start()

        sum_x(i)
        sum_chip(i + LEAD)
        start_y(i)
        start_x(i + LEAD)

        @pl.when(i == 1 - LEAD)
        def _():
            for copy in f_local:
                copy.wait()
            for copy in f_push:
                copy.wait()
            fo_own[...] = fo_own[...] + fo_par[...]
            fm_own[...] = fm_own[...] + fm_par[...]
            for copy in f_scatter:
                copy.start()
            for copy in f_state:
                copy.start()

        @pl.when(i == 3)
        def _():
            for copy in n_local:
                copy.wait()
            n_push_other.wait()
            n_push_mine.wait()
            own_no[...] = own_no[...] + par_no[...]
            n_x.start()

        @pl.when(i == 10)
        def _():
            n_x.wait()
            gn[...] = (gn[...] + pmn[...]) + xn[...]
            n_y.start()
            for copy in f_scatter:
                copy.wait()
            fo_own[keep, :] = fo_own[keep, :] + f_y[0]
            fm_own[keep, :] = fm_own[keep, :] + f_y[1]

        @pl.when(i == 20)
        def _():
            n_y.wait()
            mean = (gn[...] + yn[...]) * 0.125
            gn[...] = mean
            square = mean * mean
            total = square[:, 0:128]
            for c in range(1, NORM[1] // 128):
                total = total + square[:, c * 128:(c + 1) * 128]
            acc[0:4, :] += total

        @pl.when(i == N - LEAD)
        def _():
            f_cross.start()

        @pl.when(i == N + LAG - 2)
        def _():
            f_cross.wait()
            mean = (fm_own[keep, :] + f_x_in[...]) * 0.125
            f_out[...] = mean
            g7[6, keep_out, :] = mean
            sq_first[me] = squares(mean, WIDTH)
            f_gather.start()
            for copy in sqf_copies:
                copy.start()

        sum_y(i - LAG)
        return 0

    lax.fori_loop(1, FETCH + N + LAG, step, 0)

    sq_all[f] = acc[...]
    copies = [remote(sq_all.at[f], sq_all.at[f], sq_send.at[i], sq_recv.at[i], peer)
              for i, peer in enumerate((peer_core, peer_x, peer_diag))]
    for copy in copies:
        copy.start()

    def drain(k, _):
        on_chunk(k, lambda chunk: retire(k, chunk))
        return 0

    lax.fori_loop(N - RING, N, drain, 0)
    for copy in f_state:
        copy.wait()
    f_gather.wait()
    g7[6, give_out, :] = f_in[...]
    for copy in sqf_copies:
        copy.wait()
    total = sq_first[0]
    for i in range(1, 8):
        total = total + sq_first[i]
    for copy in copies:
        copy.wait()
    sq_out[...] = ((sq_all[0] + sq_all[1]) + (sq_all[2] + sq_all[3])) + total


def update_math(avg_scale, sq_scale, g, w, m, v, decay):
    avg = ADAM_BETA1 * m + avg_scale * g
    root = sq_scale * g
    sq = ADAM_BETA2 * v + root * root
    dev = sq * lax.rsqrt(jnp.maximum(sq, SMALLEST))
    step_dir = avg / (dev + ADAM_EPS * ROOT_TWO)
    new = (1.0 - LEARN_RATE * decay) * w - (LEARN_RATE * ROOT_TWO / BIAS_ONE) * step_dir
    return new, avg, sq, new.astype(jnp.bfloat16)


def update_kernel(sq, g7, gd, gn, w7, m7, v7, wd, md, vd, wn, mn, vn,
                  lw, lm, lv, lb, dw, dm, dv, db, nw, nm, nv, nb, ew, em, ev, eb,
                  s7w, s7m, s7v, s7b, sdw, sdm, sdv, sdb, snw, snm, snv, snb, sem7, semd, semn):
    total = jnp.sum(sq[...], keepdims=True)
    clip = jnp.minimum(1.0, 1.0 / (jnp.sqrt(total) + CLIP_EPS))
    scales = ((1.0 - ADAM_BETA1) * clip, math.sqrt(1.0 - ADAM_BETA2) * clip)

    outs = ((lw, lm, lv, lb), (dw, dm, dv, db), (nw, nm, nv, nb), (ew, em, ev, eb))
    seven_staged = (s7w, s7m, s7v, s7b)
    down_staged = (sdw, sdm, sdv, sdb)

    def layer_copies(j, row, rows):
        at = pl.ds(row, rows)
        return [pltpu.make_async_copy(src.at[j, at, :], dst.at[j, at, :], sem7.at[a, j, row // 16])
                for a, (src, dst) in enumerate(zip(seven_staged, outs[0]))]

    def embed_copies():
        return [pltpu.make_async_copy(src.at[6], dst, sem7.at[a, 6, 0])
                for a, (src, dst) in enumerate(zip(seven_staged, outs[3]))]

    def down_copies(t):
        at = pl.ds(pl.multiple_of(t * 16, 16), 16)
        return [pltpu.make_async_copy(src.at[at, :], dst.at[at, :], semd.at[a, t])
                for a, (src, dst) in enumerate(zip(down_staged, outs[1]))]

    def start(copies):
        for copy in copies:
            copy.start()

    def wait(copies):
        for copy in copies:
            copy.wait()

    def seven(j, row, decay):
        for c in range(0, WIDTH, 512):
            ix = (j, pl.ds(row, 16), pl.ds(c, 512))
            out = update_math(*scales, g7[ix], w7[ix], m7[ix], v7[ix], decay)
            for ref, val in zip(seven_staged, out):
                ref[ix] = val

    def block(j, decay):
        def rows(t, _):
            seven(j, pl.multiple_of(t * 16, 16), decay)
            return 0

        lax.fori_loop(0, 4, rows, 0)

    def first_step(t, _):
        row = pl.multiple_of(t * 16, 16)
        seven(0, row, WEIGHT_DECAY)
        start(layer_copies(0, row, 16))
        return 0

    def layer_step(j, _):
        block(j, WEIGHT_DECAY)
        start(layer_copies(j, 0, ROWS))
        return 0

    def down_step(t, _):
        row = pl.multiple_of(t * 16, 16)

        def cols(u, _):
            ix = (pl.ds(row, 16), pl.ds(pl.multiple_of(u * 1024, 1024), 1024))
            out = update_math(*scales, gd[ix], wd[ix], md[ix], vd[ix], WEIGHT_DECAY)
            for ref, val in zip(down_staged, out):
                ref[ix] = val
            return 0

        lax.fori_loop(0, FF // 1024, cols, 0)
        start(down_copies(t))
        return 0

    lax.fori_loop(0, 4, first_step, 0)
    lax.fori_loop(1, 6, layer_step, 0)
    out = update_math(*scales, gn[...], wn[...], mn[...], vn[...], WEIGHT_DECAY)
    for ref, val in zip((snw, snm, snv, snb), out):
        ref[...] = val
    norm_copies = [pltpu.make_async_copy(src, dst, semn.at[a])
                   for a, (src, dst) in enumerate(zip((snw, snm, snv, snb), outs[2]))]
    start(norm_copies)
    block(6, 0.0)
    start(embed_copies())
    lax.fori_loop(0, 4, down_step, 0)

    for row in range(0, ROWS, 16):
        wait(layer_copies(0, row, 16))

    def layer_wait(j, _):
        wait(layer_copies(j, 0, ROWS))
        return 0

    def down_wait(t, _):
        wait(down_copies(t))
        return 0

    lax.fori_loop(1, 6, layer_wait, 0)
    wait(norm_copies)
    wait(embed_copies())
    lax.fori_loop(0, 4, down_wait, 0)


def local_update(g_layer, g_down, g_norm, g_embed, layer_w, layer_m, layer_v, down_w, down_m, down_v, norm_w, norm_m,
                 norm_v, embed_w, embed_m, embed_v):
    any_spec = pl.BlockSpec(memory_space=pl.ANY)
    vmem_spec = pl.BlockSpec(memory_space=pltpu.VMEM)
    dma = pltpu.SemaphoreType.DMA
    held = [(8, 128)] + [SEVEN, DOWN, NORM] + [SEVEN] * 3 + [DOWN] * 3 + [NORM] * 3
    reduced = pl.pallas_call(
        reduce_kernel,
        out_shape=[pltpu.VMEM(shape, F32) for shape in held],
        in_specs=[any_spec] * 16,
        out_specs=[vmem_spec] * len(held),
        scratch_shapes=[pltpu.VMEM((RING, 16, WIDTH), F32), pltpu.VMEM((RING, 16, WIDTH), F32)]
        + [pltpu.VMEM(SEVEN, F32), pltpu.VMEM(DOWN, F32)] * 3
        + [pltpu.VMEM(NORM, F32)] * 5
        + [pltpu.VMEM((8, 128), F32), pltpu.VMEM((4, 8, 128), F32), pltpu.VMEM((8, 8, 128), F32)]
        + [pltpu.VMEM((8, WIDTH), F32)] + [pltpu.VMEM((FIRST, WIDTH), F32)] * 4
        + [pltpu.VMEM((2, 8, WIDTH), F32)] + [pltpu.VMEM((8, WIDTH), F32)] * 3
        + [dma((RING,)), dma((RING,)), dma((RING,)), dma((RING,)), dma((RING,)), dma((N,)), dma((RING,)), dma((N,)),
           dma((RING,)), dma((N,)), dma((3, RING)), dma((5,)), dma((4,)), dma((4,)), dma((3,)), dma((3,)),
           dma((7,)), dma((7,)), dma((7,)), dma((6,)), dma((6,)), dma,
           pltpu.SemaphoreType.REGULAR],
        compiler_params=pltpu.CompilerParams(collective_id=0, has_side_effects=True,
                                             vmem_limit_bytes=26 * 1024 * 1024),
    )(g_layer, g_down, g_norm, g_embed, layer_w, layer_m, layer_v, down_w, down_m, down_v, norm_w, norm_m, norm_v,
      embed_w, embed_m, embed_v)
    groups = ((6, ROWS, WIDTH), DOWN, NORM, (ROWS, WIDTH))
    out_shape = [jax.ShapeDtypeStruct(s, d) for s in groups for d in (F32, F32, F32, jnp.bfloat16)]
    staged = [pltpu.VMEM(s, d) for s in (SEVEN, DOWN, NORM) for d in (F32, F32, F32, jnp.bfloat16)]
    return pl.pallas_call(
        update_kernel,
        out_shape=out_shape,
        in_specs=[vmem_spec] * len(held),
        out_specs=[any_spec] * 16,
        scratch_shapes=staged + [dma((4, 7, 4)), dma((4, 4)), dma((4,))],
        compiler_params=pltpu.CompilerParams(vmem_limit_bytes=26 * 1024 * 1024),
    )(*[pltpu.with_memory_space_constraint(a, pltpu.VMEM) for a in reduced])


def solution(mesh):
    grad_four = P(("dp", "fsdp"), None, None, None)
    grad_three = P(("dp", "fsdp"), None, None)
    layer_spec = P(None, "fsdp", None)
    down_spec = P("fsdp", None)
    norm_spec = P(None, "fsdp")
    embed_spec = P("fsdp", None)
    in_specs = (grad_four, grad_three, grad_three, grad_three,
                layer_spec, layer_spec, layer_spec, down_spec, down_spec, down_spec,
                norm_spec, norm_spec, norm_spec, embed_spec, embed_spec, embed_spec)
    out_specs = (layer_spec,) * 4 + (down_spec,) * 4 + (norm_spec,) * 4 + (embed_spec,) * 4
    return jax.shard_map(local_update, mesh=mesh, in_specs=in_specs, out_specs=out_specs, check_vma=False)
```

time: 189 us -> 189 us (level)
  no operation moved by 1% of the time
where the time goes in v3:
time: 189 us
  Pallas kernels  189 us (100%)
    pallas_call x1, Pallas kernels, local_update(): pl.pallas_call(reduce_kernel, out_shape=[pltpu.VMEM(shape, F32) for shape...  178 us
    pallas_call x1, Pallas kernels, local_update(): pl.pallas_call(update_kernel, out_shape=out_shape, in_specs=[vmem_spec] *...  10.2 us

profile of v3, /device:TPU:0, one launch (start us, length us, event | category | flops | bytes accessed | tf_op | source)
XLA Modules:
  0.0 189.3 jit_solution(16252665536761693706)
XLA Ops:
  0.7 178.5 %shard_map.279 = (f32[8,128]{1,0:T(8,128)S(1)}, f32[7,64,3072]{2,1,0:T(8,128)S(1)}, f32[64,8192]{1,0:T(8,128)S(1)}, f32[4,768]{1,0:T(4,128)S(1)}, f32[7,64,3072]...) custom-call(f32[1,6,256,3072]{3,2,1,0:T(8,128)} %g_layer.1, ...), custom_call_target="tpu_custom_call" | custom-call | tf_op jit(solution)/shard_map/pallas_call | solution.py:508
  179.1 10.2 %shard_map.280 = (f32[6,64,3072]{2,1,0:T(8,128)}, f32[6,64,3072]{2,1,0:T(8,128)}, f32[6,64,3072]{2,1,0:T(8,128)}, bf16[6,64,3072]{2,1,0:T(8,128)(2,1)}, f32[64,8...) custom-call(f32[8,128]{1,0:T(8,128)S(1)} %get-tuple-element.29.sq, ...), custom_call_target="tpu_custom_call" | custom-call | tf_op jit(solution)/shard_map/pallas_call | solution.py:530

commit v4 on v3

--- a/solution.py
+++ b/solution.py
@@ -30,13 +30,16 @@
 SEVEN = (7, ROWS, WIDTH)
 DOWN = (ROWS, FF)
 
-FIRST = 16
-N_EMBED = (ROWS - FIRST) // 8
+FIRST = 8
+SPLIT = FF // 2
+N_EMBED = ROWS // 8
 N_LAYER = N_EMBED + 6 * (ROWS // 16)
 N_WIDE = N_LAYER + (FF // PIECE) * (ROWS // 16 - 1)
-N = N_WIDE + (FF // PIECE) * 2
+N = N_WIDE + (FF // PIECE) * (16 - FIRST) // 8
 
 RING = 7
+Y_RING = 8
+M_RING = 10
 FETCH = 5
 LEAD = 3
 LAG = 3
@@ -91,11 +94,24 @@
 
 
 def on_chunk(k, use):
+    if isinstance(k, int):
+        use(Chunk("embed", k))
+        return
     bounds = (0, N_EMBED, N_LAYER, N_WIDE, N)
     for i, kind in enumerate(("embed", "layer", "wide", "down")):
         @pl.when(jnp.logical_and(k >= bounds[i], k < bounds[i + 1]))
         def _():
             use(Chunk(kind, k))
+
+
+def start(copies):
+    for copy in copies:
+        copy.start()
+
+
+def wait(copies):
+    for copy in copies:
+        copy.wait()
 
 
 def squares(mean, width):
@@ -110,7 +126,7 @@
                   norm_w, norm_m, norm_v, embed_w, embed_m, embed_v,
                   sq_out, g7, gd, gn, w7, m7, v7, wd, md, vd, wn, mn, vn,
                   own_o, par_o, pm7, pmd, x7, xd, y7, yd, own_no, par_no, pmn, xn, yn, acc, sq_all, sq_first,
-                  pre, fo_own, fo_par, fm_own, fm_par, f_y, f_x_in, f_out, f_in,
+                  pre, fo_own, fo_par, f_held, f_y,
                   own_o_sem, own_m_sem, do_send, do_recv, dm_send, dm_recv, x_send, x_recv, y_send, y_recv,
                   st_sem, n_sem, n_send, n_recv, sq_send, sq_recv, sqf_send, sqf_recv, f_sem, f_send, f_recv, pre_sem, credit):
     dp = lax.axis_index("dp")
@@ -133,11 +149,11 @@
 
     def x_copy(k, chunk):
         s = lax.rem(k, RING)
-        return remote(chunk.ring(own_o, s), chunk.held(x7, xd), x_send.at[s], x_recv.at[k], peer_x)
+        return remote(chunk.ring(own_o, s), chunk.held(x7, xd), x_send.at[s], x_recv.at[s], peer_x)
 
     def y_copy(k, chunk):
         s = lax.rem(k, RING)
-        return remote(chunk.held(g7, gd), chunk.held(y7, yd), y_send.at[s], y_recv.at[k], peer_y)
+        return remote(chunk.held(g7, gd), chunk.held(y7, yd), y_send.at[s], y_recv.at[lax.rem(k, Y_RING)], peer_y)
 
     def push_other(k, chunk, source):
         s = lax.rem(k, RING)
@@ -145,7 +161,7 @@
 
     def push_mine(k, chunk, source):
         s = lax.rem(k, RING)
-        return remote(source, chunk.held(pm7, pmd), dm_send.at[s], dm_recv.at[k], peer_core)
+        return remote(source, chunk.held(pm7, pmd), dm_send.at[s], dm_recv.at[lax.rem(k, M_RING)], peer_core)
 
     def own_loads(k, chunk):
         s = lax.rem(k, RING)
@@ -164,13 +180,13 @@
             on_chunk(k - RING, lambda chunk: retire(k - RING, chunk))
             pl.semaphore_wait(credit, 1)
 
-        def start(chunk):
+        def begin(chunk):
             push_other(k, chunk, chunk.source(grads, f_diag)).start()
             for copy in own_loads(k, chunk):
                 copy.start()
             push_mine(k, chunk, chunk.source(grads, f_core)).start()
 
-        on_chunk(k, start)
+        on_chunk(k, begin)
 
     def sum_x(k):
         s = lax.rem(k, RING)
@@ -205,24 +221,18 @@
             pl.semaphore_signal(credit, inc=1, device_id=peer_core, device_id_type=MESH)
 
     def start_y(k):
-        s = lax.rem(k, RING)
-
         def use(chunk):
             y_copy(k, chunk).start()
+            seven = chunk.kind in ("embed", "layer")
             for i, (src, dst) in enumerate((((layer_w, down_w, embed_w), (w7, wd)), ((layer_m, down_m, embed_m), (m7, md)),
                                             ((layer_v, down_v, embed_v), (v7, vd)))):
-                pltpu.make_async_copy(chunk.state(*src), chunk.held(*dst), st_sem.at[i, s]).start()
+                pltpu.make_async_copy(chunk.state(*src), chunk.held(*dst), st_sem.at[i if seven else 3 + i]).start()
 
         on_chunk(k, use)
 
     def sum_y(k):
-        s = lax.rem(k, RING)
-
         def use(chunk):
             y_copy(k, chunk).wait()
-            for i, pair in enumerate(((w7, wd), (m7, md), (v7, vd))):
-                ref = chunk.held(*pair)
-                pltpu.make_async_copy(ref, ref, st_sem.at[i, s]).wait()
             mine = chunk.held(g7, gd)
             mean = (mine[...] + chunk.held(y7, yd)[...]) * 0.125
             mine[...] = mean
@@ -230,26 +240,25 @@
 
         on_chunk(k, use)
 
-    def embed_rows(q):
-        return g_embed.at[0, pl.ds(pl.multiple_of(q * ROWS + (ROWS - FIRST), 8), FIRST), :]
-
-    f_give = [pltpu.make_async_copy(embed_rows(q), own_o.at[RING - 2 + i], f_sem.at[5 + i])
-              for i, q in enumerate((f_diag, f_core))]
-    f_push = [remote(own_o.at[RING - 2], fo_par, f_send.at[0], f_recv.at[0], peer_core),
-              remote(own_o.at[RING - 1], fm_par, f_send.at[1], f_recv.at[1], peer_core)]
-    f_local = [pltpu.make_async_copy(src, dst, f_sem.at[i]) for i, (src, dst) in enumerate(
-        ((embed_rows(f_x), fo_own), (embed_rows(f), fm_own)))]
     last = pl.ds(ROWS - FIRST, FIRST)
-    f_state = [pltpu.make_async_copy(src.at[last, :], dst.at[6, last, :], f_sem.at[2 + i])
-               for i, (src, dst) in enumerate(((embed_w, w7), (embed_m, m7), (embed_v, v7)))]
-    keep = pl.ds(pl.multiple_of(dp * 8, 8), 8)
-    give = pl.ds(pl.multiple_of((1 - dp) * 8, 8), 8)
-    keep_out = pl.ds(pl.multiple_of(ROWS - FIRST + dp * 8, 8), 8)
-    give_out = pl.ds(pl.multiple_of(ROWS - FIRST + (1 - dp) * 8, 8), 8)
-    f_scatter = [remote(fo_own.at[give, :], f_y.at[0], f_send.at[2], f_recv.at[2], peer_y),
-                 remote(fm_own.at[give, :], f_y.at[1], f_send.at[3], f_recv.at[3], peer_y)]
-    f_cross = remote(fo_own.at[keep, :], f_x_in, f_send.at[4], f_recv.at[4], peer_x)
-    f_gather = remote(f_out, f_in, f_send.at[5], f_recv.at[5], peer_y)
+    keep = pl.ds(pl.multiple_of(dp * SPLIT, SPLIT), SPLIT)
+    give = pl.ds(pl.multiple_of((1 - dp) * SPLIT, SPLIT), SPLIT)
+
+    def first_rows(q):
+        return g_down.at[0, pl.ds(pl.multiple_of(q * ROWS + (ROWS - FIRST), 8), FIRST), :]
+
+    f_own, f_par = gd.at[last, :], pmd.at[last, :]
+    f_give = [pltpu.make_async_copy(first_rows(q), f_held.at[i], f_sem.at[i]) for i, q in enumerate((f_diag, f_core))]
+    f_local = [pltpu.make_async_copy(first_rows(f_x), fo_own, f_sem.at[2]),
+               pltpu.make_async_copy(first_rows(f), f_own, f_sem.at[3])]
+    f_push = [remote(f_held.at[0], fo_par, f_send.at[0], f_recv.at[0], peer_core),
+              remote(f_held.at[1], f_par, f_send.at[1], f_recv.at[1], peer_core)]
+    f_state = [pltpu.make_async_copy(src.at[last, :], dst.at[last, :], st_sem.at[3 + i])
+               for i, (src, dst) in enumerate(((down_w, wd), (down_m, md), (down_v, vd)))]
+    f_scatter = [remote(fo_own.at[:, give], f_y, f_send.at[2], f_recv.at[2], peer_y),
+                 remote(gd.at[last, give], yd.at[last, give], f_send.at[3], f_recv.at[3], peer_y)]
+    f_cross = remote(fo_own.at[:, keep], xd.at[last, keep], f_send.at[4], f_recv.at[4], peer_x)
+    f_gather = remote(gd.at[last, keep], yd.at[last, keep], f_send.at[5], f_recv.at[5], peer_y)
     me = dp * 4 + f
     sqf_copies = [remote(sq_first.at[me], sq_first.at[me], sqf_send.at[i], sqf_recv.at[i], peer)
                   for i, peer in enumerate(peers)]
@@ -283,6 +292,16 @@
         copy.wait()
         push.start()
     push_mine(0, zero, zero.source(grads, f_core)).start()
+    fetch(1)
+    fetch(2)
+    sum_chip(0)
+    start_x(0)
+    wait(f_local)
+    wait(f_push)
+    fo_own[...] = fo_own[...] + fo_par[...]
+    f_own[...] = f_own[...] + f_par[...]
+    start(f_scatter)
+    start(f_state)
 
     def step(t, _):
         i = t - FETCH
@@ -299,19 +318,6 @@
         sum_chip(i + LEAD)
         start_y(i)
         start_x(i + LEAD)
-
-        @pl.when(i == 1 - LEAD)
-        def _():
-            for copy in f_local:
-                copy.wait()
-            for copy in f_push:
-                copy.wait()
-            fo_own[...] = fo_own[...] + fo_par[...]
-            fm_own[...] = fm_own[...] + fm_par[...]
-            for copy in f_scatter:
-                copy.start()
-            for copy in f_state:
-                copy.start()
 
         @pl.when(i == 3)
         def _():
@@ -329,8 +335,8 @@
             n_y.start()
             for copy in f_scatter:
                 copy.wait()
-            fo_own[keep, :] = fo_own[keep, :] + f_y[0]
-            fm_own[keep, :] = fm_own[keep, :] + f_y[1]
+            fo_own[:, keep] = fo_own[:, keep] + f_y[...]
+            gd[last, keep] = gd[last, keep] + yd[last, keep]
 
         @pl.when(i == 20)
         def _():
@@ -350,10 +356,9 @@
         @pl.when(i == N + LAG - 2)
         def _():
             f_cross.wait()
-            mean = (fm_own[keep, :] + f_x_in[...]) * 0.125
-            f_out[...] = mean
-            g7[6, keep_out, :] = mean
-            sq_first[me] = squares(mean, WIDTH)
+            mean = (gd[last, keep] + xd[last, keep]) * 0.125
+            gd[last, keep] = mean
+            sq_first[me] = squares(mean, SPLIT)
             f_gather.start()
             for copy in sqf_copies:
                 copy.start()
@@ -361,7 +366,7 @@
         sum_y(i - LAG)
         return 0
 
-    lax.fori_loop(1, FETCH + N + LAG, step, 0)
+    lax.fori_loop(FETCH - LEAD + 1, FETCH + N + LAG, step, 0)
 
     sq_all[f] = acc[...]
     copies = [remote(sq_all.at[f], sq_all.at[f], sq_send.at[i], sq_recv.at[i], peer)
@@ -374,10 +379,10 @@
         return 0
 
     lax.fori_loop(N - RING, N, drain, 0)
-    for copy in f_state:
-        copy.wait()
+    for i, ref in enumerate((w7, m7, v7, wd, md, vd)):
+        pltpu.make_async_copy(ref, ref, st_sem.at[i]).wait()
     f_gather.wait()
-    g7[6, give_out, :] = f_in[...]
+    gd[last, give] = yd[last, give]
     for copy in sqf_copies:
         copy.wait()
     total = sq_first[0]
@@ -400,7 +405,7 @@
 
 def update_kernel(sq, g7, gd, gn, w7, m7, v7, wd, md, vd, wn, mn, vn,
                   lw, lm, lv, lb, dw, dm, dv, db, nw, nm, nv, nb, ew, em, ev, eb,
-                  s7w, s7m, s7v, s7b, sdw, sdm, sdv, sdb, snw, snm, snv, snb, sem7, semd, semn):
+                  s7w, s7m, s7v, s7b, sdw, sdm, sdv, sdb, snw, snm, snv, snb, sem):
     total = jnp.sum(sq[...], keepdims=True)
     clip = jnp.minimum(1.0, 1.0 / (jnp.sqrt(total) + CLIP_EPS))
     scales = ((1.0 - ADAM_BETA1) * clip, math.sqrt(1.0 - ADAM_BETA2) * clip)
@@ -411,25 +416,17 @@
 
     def layer_copies(j, row, rows):
         at = pl.ds(row, rows)
-        return [pltpu.make_async_copy(src.at[j, at, :], dst.at[j, at, :], sem7.at[a, j, row // 16])
+        return [pltpu.make_async_copy(src.at[j, at, :], dst.at[j, at, :], sem.at[0, a])
                 for a, (src, dst) in enumerate(zip(seven_staged, outs[0]))]
 
     def embed_copies():
-        return [pltpu.make_async_copy(src.at[6], dst, sem7.at[a, 6, 0])
+        return [pltpu.make_async_copy(src.at[6], dst, sem.at[1, a])
                 for a, (src, dst) in enumerate(zip(seven_staged, outs[3]))]
 
     def down_copies(t):
         at = pl.ds(pl.multiple_of(t * 16, 16), 16)
-        return [pltpu.make_async_copy(src.at[at, :], dst.at[at, :], semd.at[a, t])
+        return [pltpu.make_async_copy(src.at[at, :], dst.at[at, :], sem.at[2, a])
                 for a, (src, dst) in enumerate(zip(down_staged, outs[1]))]
-
-    def start(copies):
-        for copy in copies:
-            copy.start()
-
-    def wait(copies):
-        for copy in copies:
-            copy.wait()
 
     def seven(j, row, decay):
         for c in range(0, WIDTH, 512):
@@ -451,6 +448,12 @@
         start(layer_copies(0, row, 16))
         return 0
 
+    def half_step(t, _):
+        seven(1, pl.multiple_of(t * 32, 32), WEIGHT_DECAY)
+        seven(1, pl.multiple_of(t * 32 + 16, 16), WEIGHT_DECAY)
+        start(layer_copies(1, pl.multiple_of(t * 32, 32), 32))
+        return 0
+
     def layer_step(j, _):
         block(j, WEIGHT_DECAY)
         start(layer_copies(j, 0, ROWS))
@@ -471,32 +474,24 @@
         return 0
 
     lax.fori_loop(0, 4, first_step, 0)
-    lax.fori_loop(1, 6, layer_step, 0)
+    lax.fori_loop(0, 2, half_step, 0)
+    lax.fori_loop(2, 6, layer_step, 0)
     out = update_math(*scales, gn[...], wn[...], mn[...], vn[...], WEIGHT_DECAY)
     for ref, val in zip((snw, snm, snv, snb), out):
         ref[...] = val
-    norm_copies = [pltpu.make_async_copy(src, dst, semn.at[a])
+    norm_copies = [pltpu.make_async_copy(src, dst, sem.at[3, a])
                    for a, (src, dst) in enumerate(zip((snw, snm, snv, snb), outs[2]))]
     start(norm_copies)
     block(6, 0.0)
     start(embed_copies())
     lax.fori_loop(0, 4, down_step, 0)
 
-    for row in range(0, ROWS, 16):
-        wait(layer_copies(0, row, 16))
-
-    def layer_wait(j, _):
-        wait(layer_copies(j, 0, ROWS))
-        return 0
-
-    def down_wait(t, _):
-        wait(down_copies(t))
-        return 0
-
-    lax.fori_loop(1, 6, layer_wait, 0)
+    for a, staged in enumerate(seven_staged):
+        pltpu.make_async_copy(staged.at[pl.ds(0, 6)], outs[0][a], sem.at[0, a]).wait()
+    wait(embed_copies())
     wait(norm_copies)
-    wait(embed_copies())
-    lax.fori_loop(0, 4, down_wait, 0)
+    for a, staged in enumerate(down_staged):
+        pltpu.make_async_copy(staged, outs[1][a], sem.at[2, a]).wait()
 
 
 def local_update(g_layer, g_down, g_norm, g_embed, layer_w, layer_m, layer_v, down_w, down_m, down_v, norm_w, norm_m,
@@ -514,11 +509,11 @@
         + [pltpu.VMEM(SEVEN, F32), pltpu.VMEM(DOWN, F32)] * 3
         + [pltpu.VMEM(NORM, F32)] * 5
         + [pltpu.VMEM((8, 128), F32), pltpu.VMEM((4, 8, 128), F32), pltpu.VMEM((8, 8, 128), F32)]
-        + [pltpu.VMEM((8, WIDTH), F32)] + [pltpu.VMEM((FIRST, WIDTH), F32)] * 4
-        + [pltpu.VMEM((2, 8, WIDTH), F32)] + [pltpu.VMEM((8, WIDTH), F32)] * 3
-        + [dma((RING,)), dma((RING,)), dma((RING,)), dma((RING,)), dma((RING,)), dma((N,)), dma((RING,)), dma((N,)),
-           dma((RING,)), dma((N,)), dma((3, RING)), dma((5,)), dma((4,)), dma((4,)), dma((3,)), dma((3,)),
-           dma((7,)), dma((7,)), dma((7,)), dma((6,)), dma((6,)), dma,
+        + [pltpu.VMEM((8, WIDTH), F32)] + [pltpu.VMEM((FIRST, FF), F32)] * 2
+        + [pltpu.VMEM((2, FIRST, FF), F32), pltpu.VMEM((FIRST, SPLIT), F32)]
+        + [dma((RING,)), dma((RING,)), dma((RING,)), dma((RING,)), dma((RING,)), dma((M_RING,)), dma((RING,)),
+           dma((RING,)), dma((RING,)), dma((Y_RING,)), dma((6,)), dma((5,)), dma((4,)), dma((4,)), dma((3,)), dma((3,)),
+           dma((7,)), dma((7,)), dma((4,)), dma((6,)), dma((6,)), dma,
            pltpu.SemaphoreType.REGULAR],
         compiler_params=pltpu.CompilerParams(collective_id=0, has_side_effects=True,
                                              vmem_limit_bytes=26 * 1024 * 1024),
@@ -532,7 +527,7 @@
         out_shape=out_shape,
         in_specs=[vmem_spec] * len(held),
         out_specs=[any_spec] * 16,
-        scratch_shapes=staged + [dma((4, 7, 4)), dma((4, 4)), dma((4,))],
+        scratch_shapes=staged + [dma((4, 4))],
         compiler_params=pltpu.CompilerParams(vmem_limit_bytes=26 * 1024 * 1024),
     )(*[pltpu.with_memory_space_constraint(a, pltpu.VMEM) for a in reduced])
 

time: 189 us -> 186 us (0.984)
  Pallas kernels: 189 us -> 185 us
    pallas_call x1, Pallas kernels: 178 us -> 176 us  [local_update(): pl.pallas_call(reduce_kernel, out_shape=[pltpu.VMEM(shape, F32) for shape...]
where the time goes in v4:
time: 186 us
  Pallas kernels  185 us (99%)
    pallas_call x1, Pallas kernels, local_update(): pl.pallas_call(reduce_kernel, out_shape=[pltpu.VMEM(shape, F32) for shape...  176 us
    pallas_call x1, Pallas kernels, local_update(): pl.pallas_call(update_kernel, out_shape=out_shape, in_specs=[vmem_spec] *...  9.17 us

profile of v4, /device:TPU:0, one launch (start us, length us, event | category | flops | bytes accessed | tf_op | source)
XLA Modules:
  0.0 185.5 jit_solution(15884790113722910953)
XLA Ops:
  0.7 175.7 %shard_map.279 = (f32[8,128]{1,0:T(8,128)S(1)}, f32[7,64,3072]{2,1,0:T(8,128)S(1)}, f32[64,8192]{1,0:T(8,128)S(1)}, f32[4,768]{1,0:T(4,128)S(1)}, f32[7,64,3072]...) custom-call(f32[1,6,256,3072]{3,2,1,0:T(8,128)} %g_layer.1, ...), custom_call_target="tpu_custom_call" | custom-call | tf_op jit(solution)/shard_map/pallas_call | solution.py:503
  176.3 9.2 %shard_map.280 = (f32[6,64,3072]{2,1,0:T(8,128)}, f32[6,64,3072]{2,1,0:T(8,128)}, f32[6,64,3072]{2,1,0:T(8,128)}, bf16[6,64,3072]{2,1,0:T(8,128)(2,1)}, f32[64,8...) custom-call(f32[8,128]{1,0:T(8,128)S(1)} %get-tuple-element.29.sq, ...), custom_call_target="tpu_custom_call" | custom-call | tf_op jit(solution)/shard_map/pallas_call | solution.py:525

commit v5 on v4

--- a/solution.py
+++ b/solution.py
@@ -31,11 +31,13 @@
 DOWN = (ROWS, FF)
 
 FIRST = 8
-SPLIT = FF // 2
+FIRST_COLS = 8192
+SPLIT = FIRST_COLS // 2
+LAYER_ROWS = 8
 N_EMBED = ROWS // 8
-N_LAYER = N_EMBED + 6 * (ROWS // 16)
+N_LAYER = N_EMBED + 6 * (ROWS // LAYER_ROWS)
 N_WIDE = N_LAYER + (FF // PIECE) * (ROWS // 16 - 1)
-N = N_WIDE + (FF // PIECE) * (16 - FIRST) // 8
+N = N_WIDE + (FF // PIECE) * 2 - FIRST_COLS // PIECE
 
 RING = 7
 Y_RING = 8
@@ -53,9 +55,10 @@
             self.row = pl.multiple_of(k * 8, 8)
         elif kind == "layer":
             q = k - N_EMBED
-            self.rows, self.width = 16, WIDTH
-            self.j = q // 4
-            self.row = pl.multiple_of((q % 4) * 16, 16)
+            per = ROWS // LAYER_ROWS
+            self.rows, self.width = LAYER_ROWS, WIDTH
+            self.j = q // per
+            self.row = pl.multiple_of((q % per) * LAYER_ROWS, LAYER_ROWS)
         else:
             wide = kind == "wide"
             q = k - (N_LAYER if wide else N_WIDE)
@@ -241,24 +244,30 @@
         on_chunk(k, use)
 
     last = pl.ds(ROWS - FIRST, FIRST)
-    keep = pl.ds(pl.multiple_of(dp * SPLIT, SPLIT), SPLIT)
-    give = pl.ds(pl.multiple_of((1 - dp) * SPLIT, SPLIT), SPLIT)
+    keep = pl.ds(pl.multiple_of(FF - FIRST_COLS + dp * SPLIT, PIECE // 2), SPLIT)
+    give = pl.ds(pl.multiple_of(FF - FIRST_COLS + (1 - dp) * SPLIT, PIECE // 2), SPLIT)
+    cols = pl.ds(FF - FIRST_COLS, FIRST_COLS)
+    keep_o = pl.ds(pl.multiple_of(dp * SPLIT, PIECE // 2), SPLIT)
+    give_o = pl.ds(pl.multiple_of((1 - dp) * SPLIT, PIECE // 2), SPLIT)
 
     def first_rows(q):
-        return g_down.at[0, pl.ds(pl.multiple_of(q * ROWS + (ROWS - FIRST), 8), FIRST), :]
-
-    f_own, f_par = gd.at[last, :], pmd.at[last, :]
+        return g_down.at[0, pl.ds(pl.multiple_of(q * ROWS + (ROWS - FIRST), 8), FIRST), cols]
+
+    f_own = gd.at[last, cols]
     f_give = [pltpu.make_async_copy(first_rows(q), f_held.at[i], f_sem.at[i]) for i, q in enumerate((f_diag, f_core))]
     f_local = [pltpu.make_async_copy(first_rows(f_x), fo_own, f_sem.at[2]),
                pltpu.make_async_copy(first_rows(f), f_own, f_sem.at[3])]
-    f_push = [remote(f_held.at[0], fo_par, f_send.at[0], f_recv.at[0], peer_core),
-              remote(f_held.at[1], f_par, f_send.at[1], f_recv.at[1], peer_core)]
-    f_state = [pltpu.make_async_copy(src.at[last, :], dst.at[last, :], st_sem.at[3 + i])
+    f_push = []
+    for h, (half, half_o) in enumerate(((give, give_o), (keep, keep_o))):
+        for i, ref in enumerate((fo_par.at[:, half_o], pmd.at[last, half])):
+            f_push.append(remote(f_held.at[i, :, half_o], ref, f_send.at[4 + 2 * h + i], f_recv.at[4 + 2 * h + i],
+                                 peer_core))
+    f_state = [pltpu.make_async_copy(src.at[last, cols], dst.at[last, cols], st_sem.at[3 + i])
                for i, (src, dst) in enumerate(((down_w, wd), (down_m, md), (down_v, vd)))]
-    f_scatter = [remote(fo_own.at[:, give], f_y, f_send.at[2], f_recv.at[2], peer_y),
-                 remote(gd.at[last, give], yd.at[last, give], f_send.at[3], f_recv.at[3], peer_y)]
-    f_cross = remote(fo_own.at[:, keep], xd.at[last, keep], f_send.at[4], f_recv.at[4], peer_x)
-    f_gather = remote(gd.at[last, keep], yd.at[last, keep], f_send.at[5], f_recv.at[5], peer_y)
+    f_scatter = [remote(fo_own.at[:, give_o], f_y, f_send.at[0], f_recv.at[0], peer_y),
+                 remote(gd.at[last, give], yd.at[last, give], f_send.at[1], f_recv.at[1], peer_y)]
+    f_cross = remote(fo_own.at[:, keep_o], xd.at[last, keep], f_send.at[2], f_recv.at[2], peer_x)
+    f_gather = remote(gd.at[last, keep], yd.at[last, keep], f_send.at[3], f_recv.at[3], peer_y)
     me = dp * 4 + f
     sqf_copies = [remote(sq_first.at[me], sq_first.at[me], sqf_send.at[i], sqf_recv.at[i], peer)
                   for i, peer in enumerate(peers)]
@@ -283,24 +292,30 @@
     acc[...] = jnp.zeros_like(acc)
 
     barrier = pltpu.get_barrier_semaphore()
-    for peer in peers:
+    near = (peer_core, peer_x, peer_y)
+    for peer in near:
         pl.semaphore_signal(barrier, inc=1, device_id=peer, device_id_type=MESH)
+    wait(f_give)
+    pl.semaphore_wait(barrier, len(near))
+    start(f_push[:2])
     ahead.wait()
-    pl.semaphore_wait(barrier, len(peers))
     push_other(0, zero, pre).start()
-    for copy, push in zip(f_give, f_push):
-        copy.wait()
-        push.start()
+    start(f_push[2:])
     push_mine(0, zero, zero.source(grads, f_core)).start()
     fetch(1)
     fetch(2)
+    wait(f_local)
+    wait(f_push[:1])
+    fo_own[:, give_o] = fo_own[:, give_o] + fo_par[:, give_o]
+    f_scatter[0].start()
+    wait(f_push[1:2])
+    gd[last, give] = gd[last, give] + pmd[last, give]
+    f_scatter[1].start()
     sum_chip(0)
     start_x(0)
-    wait(f_local)
-    wait(f_push)
-    fo_own[...] = fo_own[...] + fo_par[...]
-    f_own[...] = f_own[...] + f_par[...]
-    start(f_scatter)
+    wait(f_push[2:])
+    fo_own[:, keep_o] = fo_own[:, keep_o] + fo_par[:, keep_o]
+    gd[last, keep] = gd[last, keep] + pmd[last, keep]
     start(f_state)
 
     def step(t, _):
@@ -335,7 +350,7 @@
             n_y.start()
             for copy in f_scatter:
                 copy.wait()
-            fo_own[:, keep] = fo_own[:, keep] + f_y[...]
+            fo_own[:, keep_o] = fo_own[:, keep_o] + f_y[...]
             gd[last, keep] = gd[last, keep] + yd[last, keep]
 
         @pl.when(i == 20)
@@ -359,9 +374,8 @@
             mean = (gd[last, keep] + xd[last, keep]) * 0.125
             gd[last, keep] = mean
             sq_first[me] = squares(mean, SPLIT)
+            start(sqf_copies)
             f_gather.start()
-            for copy in sqf_copies:
-                copy.start()
 
         sum_y(i - LAG)
         return 0
@@ -509,11 +523,11 @@
         + [pltpu.VMEM(SEVEN, F32), pltpu.VMEM(DOWN, F32)] * 3
         + [pltpu.VMEM(NORM, F32)] * 5
         + [pltpu.VMEM((8, 128), F32), pltpu.VMEM((4, 8, 128), F32), pltpu.VMEM((8, 8, 128), F32)]
-        + [pltpu.VMEM((8, WIDTH), F32)] + [pltpu.VMEM((FIRST, FF), F32)] * 2
-        + [pltpu.VMEM((2, FIRST, FF), F32), pltpu.VMEM((FIRST, SPLIT), F32)]
+        + [pltpu.VMEM((8, WIDTH), F32)] + [pltpu.VMEM((FIRST, FIRST_COLS), F32)] * 2
+        + [pltpu.VMEM((2, FIRST, FIRST_COLS), F32), pltpu.VMEM((FIRST, SPLIT), F32)]
         + [dma((RING,)), dma((RING,)), dma((RING,)), dma((RING,)), dma((RING,)), dma((M_RING,)), dma((RING,)),
            dma((RING,)), dma((RING,)), dma((Y_RING,)), dma((6,)), dma((5,)), dma((4,)), dma((4,)), dma((3,)), dma((3,)),
-           dma((7,)), dma((7,)), dma((4,)), dma((6,)), dma((6,)), dma,
+           dma((7,)), dma((7,)), dma((4,)), dma((8,)), dma((8,)), dma,
            pltpu.SemaphoreType.REGULAR],
         compiler_params=pltpu.CompilerParams(collective_id=0, has_side_effects=True,
                                              vmem_limit_bytes=26 * 1024 * 1024),

time: 186 us -> 185 us (level)
  no operation moved by 1% of the time
where the time goes in v5:
time: 185 us
  Pallas kernels  184 us (99%)
    pallas_call x1, Pallas kernels, local_update(): pl.pallas_call(reduce_kernel, out_shape=[pltpu.VMEM(shape, F32) for shape...  175 us
    pallas_call x1, Pallas kernels, local_update(): pl.pallas_call(update_kernel, out_shape=out_shape, in_specs=[vmem_spec] *...  9.17 us

profile of v5, /device:TPU:0, one launch (start us, length us, event | category | flops | bytes accessed | tf_op | source)
XLA Modules:
  0.0 184.5 jit_solution(12528545094393548511)
XLA Ops:
  0.7 174.7 %shard_map.279 = (f32[8,128]{1,0:T(8,128)S(1)}, f32[7,64,3072]{2,1,0:T(8,128)S(1)}, f32[64,8192]{1,0:T(8,128)S(1)}, f32[4,768]{1,0:T(4,128)S(1)}, f32[7,64,3072]...) custom-call(f32[1,6,256,3072]{3,2,1,0:T(8,128)} %g_layer.1, ...), custom_call_target="tpu_custom_call" | custom-call | tf_op jit(solution)/shard_map/pallas_call | solution.py:517
  175.4 9.2 %shard_map.280 = (f32[6,64,3072]{2,1,0:T(8,128)}, f32[6,64,3072]{2,1,0:T(8,128)}, f32[6,64,3072]{2,1,0:T(8,128)}, bf16[6,64,3072]{2,1,0:T(8,128)(2,1)}, f32[64,8...) custom-call(f32[8,128]{1,0:T(8,128)S(1)} %get-tuple-element.29.sq, ...), custom_call_target="tpu_custom_call" | custom-call | tf_op jit(solution)/shard_map/pallas_call | solution.py:539

commit v6 on v5

--- a/solution.py
+++ b/solution.py
@@ -31,77 +31,69 @@
 DOWN = (ROWS, FF)
 
 FIRST = 8
-FIRST_COLS = 8192
+FIRST_COLS = 6144
 SPLIT = FIRST_COLS // 2
-LAYER_ROWS = 8
-N_EMBED = ROWS // 8
-N_LAYER = N_EMBED + 6 * (ROWS // LAYER_ROWS)
-N_WIDE = N_LAYER + (FF // PIECE) * (ROWS // 16 - 1)
-N = N_WIDE + (FF // PIECE) * 2 - FIRST_COLS // PIECE
-
-RING = 7
-Y_RING = 8
-M_RING = 10
-FETCH = 5
-LEAD = 3
-LAG = 3
+PART = 1536
+BLOCK = (ROWS // 8) * (WIDTH // PART)
+N_EMBED = BLOCK
+N_LAYER = N_EMBED + 6 * BLOCK
+N = N_LAYER + (FF // PIECE) * (ROWS // 8) - FIRST_COLS // PIECE
+
+LEAD = 4
+FETCH = 7
+RING = 9
+LAG = 5
+Y_RING = 2 * LAG + 2
+M_RING = RING + LEAD
 
 
 class Chunk:
     def __init__(self, kind, k):
         self.kind = kind
-        if kind == "embed":
-            self.rows, self.width = 8, WIDTH
-            self.row = pl.multiple_of(k * 8, 8)
-        elif kind == "layer":
-            q = k - N_EMBED
-            per = ROWS // LAYER_ROWS
-            self.rows, self.width = LAYER_ROWS, WIDTH
-            self.j = q // per
-            self.row = pl.multiple_of((q % per) * LAYER_ROWS, LAYER_ROWS)
+        if kind == "down":
+            q = k - N_LAYER
+            per = FF // PIECE
+            self.width = PIECE
         else:
-            wide = kind == "wide"
-            q = k - (N_LAYER if wide else N_WIDE)
-            self.rows, self.width = (16, PIECE) if wide else (8, PIECE)
-            start = 0 if wide else ROWS - 16
-            self.row = pl.multiple_of(start + (q // 4) * self.rows, 8)
-            self.cols = pl.ds(pl.multiple_of((q % 4) * PIECE, PIECE), PIECE)
+            q = k if kind == "embed" else (k - N_EMBED) % BLOCK
+            per = WIDTH // PART
+            self.width = PART
+            self.j = 6 if kind == "embed" else (k - N_EMBED) // BLOCK
+        self.row = pl.multiple_of((q // per) * 8, 8)
+        self.rows = pl.ds(self.row, 8)
+        self.cols = pl.ds(pl.multiple_of((q % per) * self.width, 512), self.width)
 
     def source(self, grads, q):
         g_layer, g_down, g_embed = grads
-        rows = pl.ds(pl.multiple_of(q * ROWS + self.row, 8), self.rows)
+        rows = pl.ds(pl.multiple_of(q * ROWS + self.row, 8), 8)
         if self.kind == "embed":
-            return g_embed.at[0, rows, :]
+            return g_embed.at[0, rows, self.cols]
         if self.kind == "layer":
-            return g_layer.at[0, self.j, rows, :]
+            return g_layer.at[0, self.j, rows, self.cols]
         return g_down.at[0, rows, self.cols]
 
     def state(self, layer, down, embed):
-        rows = pl.ds(self.row, self.rows)
         if self.kind == "embed":
-            return embed.at[rows, :]
+            return embed.at[self.rows, self.cols]
         if self.kind == "layer":
-            return layer.at[self.j, rows, :]
-        return down.at[rows, self.cols]
+            return layer.at[self.j, self.rows, self.cols]
+        return down.at[self.rows, self.cols]
 
     def held(self, seven, down):
-        rows = pl.ds(self.row, self.rows)
-        if self.kind == "embed":
-            return seven.at[6, rows, :]
-        if self.kind == "layer":
-            return seven.at[self.j, rows, :]
-        return down.at[rows, self.cols]
+        if self.kind == "down":
+            return down.at[self.rows, self.cols]
+        return seven.at[self.j, self.rows, self.cols]
 
     def ring(self, ring, s):
-        return ring.at[s, pl.ds(0, self.rows), pl.ds(0, self.width)]
+        return ring.at[s, :, pl.ds(0, self.width)]
 
 
 def on_chunk(k, use):
     if isinstance(k, int):
         use(Chunk("embed", k))
         return
-    bounds = (0, N_EMBED, N_LAYER, N_WIDE, N)
-    for i, kind in enumerate(("embed", "layer", "wide", "down")):
+    bounds = (0, N_EMBED, N_LAYER, N)
+    for i, kind in enumerate(("embed", "layer", "down")):
         @pl.when(jnp.logical_and(k >= bounds[i], k < bounds[i + 1]))
         def _():
             use(Chunk(kind, k))
@@ -302,8 +294,8 @@
     push_other(0, zero, pre).start()
     start(f_push[2:])
     push_mine(0, zero, zero.source(grads, f_core)).start()
-    fetch(1)
-    fetch(2)
+    for k in range(1, FETCH - LEAD + 1):
+        fetch(k)
     wait(f_local)
     wait(f_push[:1])
     fo_own[:, give_o] = fo_own[:, give_o] + fo_par[:, give_o]
@@ -519,11 +511,11 @@
         out_shape=[pltpu.VMEM(shape, F32) for shape in held],
         in_specs=[any_spec] * 16,
         out_specs=[vmem_spec] * len(held),
-        scratch_shapes=[pltpu.VMEM((RING, 16, WIDTH), F32), pltpu.VMEM((RING, 16, WIDTH), F32)]
+        scratch_shapes=[pltpu.VMEM((RING, 8, max(PART, PIECE)), F32)] * 2
         + [pltpu.VMEM(SEVEN, F32), pltpu.VMEM(DOWN, F32)] * 3
         + [pltpu.VMEM(NORM, F32)] * 5
         + [pltpu.VMEM((8, 128), F32), pltpu.VMEM((4, 8, 128), F32), pltpu.VMEM((8, 8, 128), F32)]
-        + [pltpu.VMEM((8, WIDTH), F32)] + [pltpu.VMEM((FIRST, FIRST_COLS), F32)] * 2
+        + [pltpu.VMEM((8, PART), F32)] + [pltpu.VMEM((FIRST, FIRST_COLS), F32)] * 2
         + [pltpu.VMEM((2, FIRST, FIRST_COLS), F32), pltpu.VMEM((FIRST, SPLIT), F32)]
         + [dma((RING,)), dma((RING,)), dma((RING,)), dma((RING,)), dma((RING,)), dma((M_RING,)), dma((RING,)),
            dma((RING,)), dma((RING,)), dma((Y_RING,)), dma((6,)), dma((5,)), dma((4,)), dma((4,)), dma((3,)), dma((3,)),

time: 185 us -> 184 us (level)
  no operation moved by 1% of the time
where the time goes in v6:
time: 184 us
  Pallas kernels  184 us (100%)
    pallas_call x1, Pallas kernels, local_update(): pl.pallas_call(reduce_kernel, out_shape=[pltpu.VMEM(shape, F32) for shape...  174 us
    pallas_call x1, Pallas kernels, local_update(): pl.pallas_call(update_kernel, out_shape=out_shape, in_specs=[vmem_spec] *...  9.17 us

profile of v6, /device:TPU:0, one launch (start us, length us, event | category | flops | bytes accessed | tf_op | source)
XLA Modules:
  0.0 184.3 jit_solution(6904795158172376327)
XLA Ops:
  0.7 174.4 %shard_map.279 = (f32[8,128]{1,0:T(8,128)S(1)}, f32[7,64,3072]{2,1,0:T(8,128)S(1)}, f32[64,8192]{1,0:T(8,128)S(1)}, f32[4,768]{1,0:T(4,128)S(1)}, f32[7,64,3072]...) custom-call(f32[1,6,256,3072]{3,2,1,0:T(8,128)} %g_layer.1, ...), custom_call_target="tpu_custom_call" | custom-call | tf_op jit(solution)/shard_map/pallas_call | solution.py:509
  175.1 9.2 %shard_map.280 = (f32[6,64,3072]{2,1,0:T(8,128)}, f32[6,64,3072]{2,1,0:T(8,128)}, f32[6,64,3072]{2,1,0:T(8,128)}, bf16[6,64,3072]{2,1,0:T(8,128)(2,1)}, f32[64,8...) custom-call(f32[8,128]{1,0:T(8,128)S(1)} %get-tuple-element.29.sq, ...), custom_call_target="tpu_custom_call" | custom-call | tf_op jit(solution)/shard_map/pallas_call | solution.py:531

commit v7 on v6

--- a/solution.py
+++ b/solution.py
@@ -109,6 +109,10 @@
         copy.wait()
 
 
+def take(ref, sem):
+    pltpu.make_async_copy(ref, ref, sem).wait()
+
+
 def squares(mean, width):
     parts = [mean[r:r + 8, i * 128:(i + 1) * 128] for r in range(0, mean.shape[0], 8) for i in range(width // 128)]
     sums = [p * p for p in parts[:4]]
@@ -122,8 +126,7 @@
                   sq_out, g7, gd, gn, w7, m7, v7, wd, md, vd, wn, mn, vn,
                   own_o, par_o, pm7, pmd, x7, xd, y7, yd, own_no, par_no, pmn, xn, yn, acc, sq_all, sq_first,
                   pre, fo_own, fo_par, f_held, f_y,
-                  own_o_sem, own_m_sem, do_send, do_recv, dm_send, dm_recv, x_send, x_recv, y_send, y_recv,
-                  st_sem, n_sem, n_send, n_recv, sq_send, sq_recv, sqf_send, sqf_recv, f_sem, f_send, f_recv, pre_sem, credit):
+                  out_sem, other_sem, mine_sem, y_sem, st_sem, n_sem, sq_sem, f_sem, pre_sem, credit):
     dp = lax.axis_index("dp")
     f = lax.axis_index("fsdp")
     core = lax.rem(f, 2)
@@ -144,30 +147,30 @@
 
     def x_copy(k, chunk):
         s = lax.rem(k, RING)
-        return remote(chunk.ring(own_o, s), chunk.held(x7, xd), x_send.at[s], x_recv.at[s], peer_x)
+        return remote(chunk.ring(own_o, s), chunk.held(x7, xd), out_sem.at[s], mine_sem.at[lax.rem(k, M_RING)], peer_x)
 
     def y_copy(k, chunk):
-        s = lax.rem(k, RING)
-        return remote(chunk.held(g7, gd), chunk.held(y7, yd), y_send.at[s], y_recv.at[lax.rem(k, Y_RING)], peer_y)
+        sem = y_sem.at[lax.rem(k, Y_RING)]
+        return remote(chunk.held(g7, gd), chunk.held(y7, yd), sem, sem, peer_y)
 
     def push_other(k, chunk, source):
         s = lax.rem(k, RING)
-        return remote(source, chunk.ring(par_o, s), do_send.at[s], do_recv.at[s], peer_core)
+        return remote(source, chunk.ring(par_o, s), out_sem.at[s], other_sem.at[s], peer_core)
 
     def push_mine(k, chunk, source):
         s = lax.rem(k, RING)
-        return remote(source, chunk.held(pm7, pmd), dm_send.at[s], dm_recv.at[lax.rem(k, M_RING)], peer_core)
+        return remote(source, chunk.held(pm7, pmd), out_sem.at[s], mine_sem.at[lax.rem(k, M_RING)], peer_core)
 
     def own_loads(k, chunk):
         s = lax.rem(k, RING)
-        return [pltpu.make_async_copy(chunk.source(grads, f_x), chunk.ring(own_o, s), own_o_sem.at[s]),
-                pltpu.make_async_copy(chunk.source(grads, f), chunk.held(g7, gd), own_m_sem.at[s])]
+        return [pltpu.make_async_copy(chunk.source(grads, f_x), chunk.ring(own_o, s), other_sem.at[s]),
+                pltpu.make_async_copy(chunk.source(grads, f), chunk.held(g7, gd), mine_sem.at[lax.rem(k, M_RING)])]
+
+    def times(count, chunk):
+        return own_o.at[pl.ds(0, count), :, pl.ds(0, chunk.width)]
 
     def retire(k, chunk):
-        s = lax.rem(k, RING)
-        x_copy(k, chunk).wait_send()
-        push_other(k, chunk, chunk.ring(par_o, s)).wait_send()
-        push_mine(k, chunk, chunk.held(pm7, pmd)).wait_send()
+        take(times(3, chunk), out_sem.at[lax.rem(k, RING)])
 
     def fetch(k):
         @pl.when(jnp.logical_and(k >= RING, k < N))
@@ -184,14 +187,10 @@
         on_chunk(k, begin)
 
     def sum_x(k):
-        s = lax.rem(k, RING)
-
         def use(chunk):
+            take(times(3, chunk), mine_sem.at[lax.rem(k, M_RING)])
             mine = chunk.held(g7, gd)
             theirs = chunk.held(pm7, pmd)
-            pltpu.make_async_copy(mine, mine, own_m_sem.at[s]).wait()
-            push_mine(k, chunk, theirs).wait_recv()
-            x_copy(k, chunk).wait_recv()
             mine[...] = (mine[...] + theirs[...]) + chunk.held(x7, xd)[...]
 
         on_chunk(k, use)
@@ -202,8 +201,7 @@
         def use(chunk):
             mine = chunk.ring(own_o, s)
             theirs = chunk.ring(par_o, s)
-            pltpu.make_async_copy(mine, mine, own_o_sem.at[s]).wait()
-            push_other(k, chunk, theirs).wait_recv()
+            take(times(2, chunk), other_sem.at[s])
             mine[...] = mine[...] + theirs[...]
 
         on_chunk(k, use)
@@ -227,7 +225,7 @@
 
     def sum_y(k):
         def use(chunk):
-            y_copy(k, chunk).wait()
+            take(times(2, chunk), y_sem.at[lax.rem(k, Y_RING)])
             mine = chunk.held(g7, gd)
             mean = (mine[...] + chunk.held(y7, yd)[...]) * 0.125
             mine[...] = mean
@@ -246,33 +244,37 @@
         return g_down.at[0, pl.ds(pl.multiple_of(q * ROWS + (ROWS - FIRST), 8), FIRST), cols]
 
     f_own = gd.at[last, cols]
-    f_give = [pltpu.make_async_copy(first_rows(q), f_held.at[i], f_sem.at[i]) for i, q in enumerate((f_diag, f_core))]
-    f_local = [pltpu.make_async_copy(first_rows(f_x), fo_own, f_sem.at[2]),
-               pltpu.make_async_copy(first_rows(f), f_own, f_sem.at[3])]
+    f_give = [pltpu.make_async_copy(first_rows(q), f_held.at[i], f_sem.at[0]) for i, q in enumerate((f_diag, f_core))]
+    f_local = [pltpu.make_async_copy(first_rows(f_x), fo_own, f_sem.at[1]),
+               pltpu.make_async_copy(first_rows(f), f_own, f_sem.at[1])]
     f_push = []
     for h, (half, half_o) in enumerate(((give, give_o), (keep, keep_o))):
         for i, ref in enumerate((fo_par.at[:, half_o], pmd.at[last, half])):
-            f_push.append(remote(f_held.at[i, :, half_o], ref, f_send.at[4 + 2 * h + i], f_recv.at[4 + 2 * h + i],
-                                 peer_core))
+            f_push.append(remote(f_held.at[i, :, half_o], ref, f_sem.at[2],
+                                 f_sem.at[3 + i] if h == 0 else f_sem.at[5], peer_core))
     f_state = [pltpu.make_async_copy(src.at[last, cols], dst.at[last, cols], st_sem.at[3 + i])
                for i, (src, dst) in enumerate(((down_w, wd), (down_m, md), (down_v, vd)))]
-    f_scatter = [remote(fo_own.at[:, give_o], f_y, f_send.at[0], f_recv.at[0], peer_y),
-                 remote(gd.at[last, give], yd.at[last, give], f_send.at[1], f_recv.at[1], peer_y)]
-    f_cross = remote(fo_own.at[:, keep_o], xd.at[last, keep], f_send.at[2], f_recv.at[2], peer_x)
-    f_gather = remote(gd.at[last, keep], yd.at[last, keep], f_send.at[3], f_recv.at[3], peer_y)
+    f_scatter = [remote(fo_own.at[:, give_o], f_y, f_sem.at[6], f_sem.at[6], peer_y),
+                 remote(gd.at[last, give], yd.at[last, give], f_sem.at[6], f_sem.at[6], peer_y)]
+    f_cross = remote(fo_own.at[:, keep_o], xd.at[last, keep], f_sem.at[7], f_sem.at[7], peer_x)
+    f_gather = remote(gd.at[last, keep], yd.at[last, keep], f_sem.at[8], f_sem.at[8], peer_y)
     me = dp * 4 + f
-    sqf_copies = [remote(sq_first.at[me], sq_first.at[me], sqf_send.at[i], sqf_recv.at[i], peer)
-                  for i, peer in enumerate(peers)]
+    sqf_copies = [remote(sq_first.at[me], sq_first.at[me], sq_sem.at[0], sq_sem.at[1], peer)
+                  for peer in peers]
 
     def norm_source(q):
         return g_norm.at[0, :, pl.ds(pl.multiple_of(q * NORM[1], 128), NORM[1])]
 
-    n_push_other = remote(norm_source(f_diag), par_no, n_send.at[0], n_recv.at[0], peer_core)
-    n_push_mine = remote(norm_source(f_core), pmn, n_send.at[1], n_recv.at[1], peer_core)
-    n_x = remote(own_no, xn, n_send.at[2], n_recv.at[2], peer_x)
-    n_y = remote(gn, yn, n_send.at[3], n_recv.at[3], peer_y)
-    n_local = [pltpu.make_async_copy(src, dst, n_sem.at[i]) for i, (src, dst) in enumerate(
-        ((norm_source(f_x), own_no), (norm_source(f), gn), (norm_w, wn), (norm_m, mn), (norm_v, vn)))]
+    n_push_other = remote(norm_source(f_diag), par_no, n_sem.at[1], n_sem.at[0], peer_core)
+    n_push_mine = remote(norm_source(f_core), pmn, n_sem.at[1], n_sem.at[0], peer_core)
+    n_x = remote(own_no, xn, n_sem.at[2], n_sem.at[2], peer_x)
+    n_y = remote(gn, yn, n_sem.at[3], n_sem.at[3], peer_y)
+    n_local = [pltpu.make_async_copy(src, dst, n_sem.at[0]) for src, dst in
+               ((norm_source(f_x), own_no), (norm_source(f), gn), (norm_w, wn), (norm_m, mn), (norm_v, vn))]
+
+    def n_times(count):
+        return fo_par.at[:, pl.ds(0, count * NORM[0] * NORM[1] // 8)]
+
 
     zero = Chunk("embed", 0)
     ahead = pltpu.make_async_copy(zero.source(grads, f_diag), pre, pre_sem)
@@ -287,7 +289,7 @@
     near = (peer_core, peer_x, peer_y)
     for peer in near:
         pl.semaphore_signal(barrier, inc=1, device_id=peer, device_id_type=MESH)
-    wait(f_give)
+    take(f_held, f_sem.at[0])
     pl.semaphore_wait(barrier, len(near))
     start(f_push[:2])
     ahead.wait()
@@ -296,16 +298,17 @@
     push_mine(0, zero, zero.source(grads, f_core)).start()
     for k in range(1, FETCH - LEAD + 1):
         fetch(k)
-    wait(f_local)
-    wait(f_push[:1])
+    take(f_held, f_sem.at[1])
+    take(fo_par.at[:, give_o], f_sem.at[3])
     fo_own[:, give_o] = fo_own[:, give_o] + fo_par[:, give_o]
     f_scatter[0].start()
-    wait(f_push[1:2])
+    take(fo_par.at[:, give_o], f_sem.at[4])
     gd[last, give] = gd[last, give] + pmd[last, give]
     f_scatter[1].start()
     sum_chip(0)
     start_x(0)
-    wait(f_push[2:])
+    take(fo_par, f_sem.at[5])
+    take(f_held, f_sem.at[2])
     fo_own[:, keep_o] = fo_own[:, keep_o] + fo_par[:, keep_o]
     gd[last, keep] = gd[last, keep] + pmd[last, keep]
     start(f_state)
@@ -328,26 +331,23 @@
 
         @pl.when(i == 3)
         def _():
-            for copy in n_local:
-                copy.wait()
-            n_push_other.wait()
-            n_push_mine.wait()
+            take(n_times(7), n_sem.at[0])
+            take(n_times(2), n_sem.at[1])
             own_no[...] = own_no[...] + par_no[...]
             n_x.start()
 
         @pl.when(i == 10)
         def _():
-            n_x.wait()
+            take(n_times(2), n_sem.at[2])
             gn[...] = (gn[...] + pmn[...]) + xn[...]
             n_y.start()
-            for copy in f_scatter:
-                copy.wait()
+            take(f_held, f_sem.at[6])
             fo_own[:, keep_o] = fo_own[:, keep_o] + f_y[...]
             gd[last, keep] = gd[last, keep] + yd[last, keep]
 
         @pl.when(i == 20)
         def _():
-            n_y.wait()
+            take(n_times(2), n_sem.at[3])
             mean = (gn[...] + yn[...]) * 0.125
             gn[...] = mean
             square = mean * mean
@@ -360,9 +360,9 @@
         def _():
             f_cross.start()
 
-        @pl.when(i == N + LAG - 2)
-        def _():
-            f_cross.wait()
+        @pl.when(i == N + LAG - 3)
+        def _():
+            take(fo_par, f_sem.at[7])
             mean = (gd[last, keep] + xd[last, keep]) * 0.125
             gd[last, keep] = mean
             sq_first[me] = squares(mean, SPLIT)
@@ -375,8 +375,8 @@
     lax.fori_loop(FETCH - LEAD + 1, FETCH + N + LAG, step, 0)
 
     sq_all[f] = acc[...]
-    copies = [remote(sq_all.at[f], sq_all.at[f], sq_send.at[i], sq_recv.at[i], peer)
-              for i, peer in enumerate((peer_core, peer_x, peer_diag))]
+    copies = [remote(sq_all.at[f], sq_all.at[f], sq_sem.at[2], sq_sem.at[3], peer)
+              for peer in (peer_core, peer_x, peer_diag)]
     for copy in copies:
         copy.start()
 
@@ -387,15 +387,15 @@
     lax.fori_loop(N - RING, N, drain, 0)
     for i, ref in enumerate((w7, m7, v7, wd, md, vd)):
         pltpu.make_async_copy(ref, ref, st_sem.at[i]).wait()
-    f_gather.wait()
+    take(fo_par, f_sem.at[8])
     gd[last, give] = yd[last, give]
-    for copy in sqf_copies:
-        copy.wait()
+    take(sq_first.at[pl.ds(0, 7)], sq_sem.at[0])
+    take(sq_first.at[pl.ds(0, 7)], sq_sem.at[1])
     total = sq_first[0]
     for i in range(1, 8):
         total = total + sq_first[i]
-    for copy in copies:
-        copy.wait()
+    take(sq_all.at[pl.ds(0, 3)], sq_sem.at[2])
+    take(sq_all.at[pl.ds(0, 3)], sq_sem.at[3])
     sq_out[...] = ((sq_all[0] + sq_all[1]) + (sq_all[2] + sq_all[3])) + total
 
 
@@ -517,9 +517,7 @@
         + [pltpu.VMEM((8, 128), F32), pltpu.VMEM((4, 8, 128), F32), pltpu.VMEM((8, 8, 128), F32)]
         + [pltpu.VMEM((8, PART), F32)] + [pltpu.VMEM((FIRST, FIRST_COLS), F32)] * 2
         + [pltpu.VMEM((2, FIRST, FIRST_COLS), F32), pltpu.VMEM((FIRST, SPLIT), F32)]
-        + [dma((RING,)), dma((RING,)), dma((RING,)), dma((RING,)), dma((RING,)), dma((M_RING,)), dma((RING,)),
-           dma((RING,)), dma((RING,)), dma((Y_RING,)), dma((6,)), dma((5,)), dma((4,)), dma((4,)), dma((3,)), dma((3,)),
-           dma((7,)), dma((7,)), dma((4,)), dma((8,)), dma((8,)), dma,
+        + [dma((RING,)), dma((RING,)), dma((M_RING,)), dma((Y_RING,)), dma((6,)), dma((4,)), dma((4,)), dma((9,)), dma,
            pltpu.SemaphoreType.REGULAR],
         compiler_params=pltpu.CompilerParams(collective_id=0, has_side_effects=True,
                                              vmem_limit_bytes=26 * 1024 * 1024),

time: 184 us -> 183 us (level)
  no operation moved by 1% of the time
where the time goes in v7:
time: 183 us
  Pallas kernels  183 us (100%)
    pallas_call x1, Pallas kernels, local_update(): pl.pallas_call(reduce_kernel, out_shape=[pltpu.VMEM(shape, F32) for shape...  173 us
    pallas_call x1, Pallas kernels, local_update(): pl.pallas_call(update_kernel, out_shape=out_shape, in_specs=[vmem_spec] *...  9.17 us

profile of v7, /device:TPU:0, one launch (start us, length us, event | category | flops | bytes accessed | tf_op | source)
XLA Modules:
  0.0 183.3 jit_solution(9575956469737110203)
XLA Ops:
  0.7 173.5 %shard_map.279 = (f32[8,128]{1,0:T(8,128)S(1)}, f32[7,64,3072]{2,1,0:T(8,128)S(1)}, f32[64,8192]{1,0:T(8,128)S(1)}, f32[4,768]{1,0:T(4,128)S(1)}, f32[7,64,3072]...) custom-call(f32[1,6,256,3072]{3,2,1,0:T(8,128)} %g_layer.1, ...), custom_call_target="tpu_custom_call" | custom-call | tf_op jit(solution)/shard_map/pallas_call | solution.py:509
  174.1 9.2 %shard_map.280 = (f32[6,64,3072]{2,1,0:T(8,128)}, f32[6,64,3072]{2,1,0:T(8,128)}, f32[6,64,3072]{2,1,0:T(8,128)}, bf16[6,64,3072]{2,1,0:T(8,128)(2,1)}, f32[64,8...) custom-call(f32[8,128]{1,0:T(8,128)S(1)} %get-tuple-element.29.sq, ...), custom_call_target="tpu_custom_call" | custom-call | tf_op jit(solution)/shard_map/pallas_call | solution.py:529

commit v8 on v7

--- a/solution.py
+++ b/solution.py
@@ -25,21 +25,22 @@
 ROWS = 64
 WIDTH = 3072
 FF = 8192
-PIECE = 2048
+PIECE = 1024
 NORM = (4, 768)
 SEVEN = (7, ROWS, WIDTH)
 DOWN = (ROWS, FF)
 
 FIRST = 8
-FIRST_COLS = 6144
+FIRST_COLS = 5120
 SPLIT = FIRST_COLS // 2
 PART = 1536
 BLOCK = (ROWS // 8) * (WIDTH // PART)
 N_EMBED = BLOCK
 N_LAYER = N_EMBED + 6 * BLOCK
+N_HALF = 3
 N = N_LAYER + (FF // PIECE) * (ROWS // 8) - FIRST_COLS // PIECE
 
-LEAD = 4
+LEAD = 5
 FETCH = 7
 RING = 9
 LAG = 5
@@ -50,7 +51,7 @@
 class Chunk:
     def __init__(self, kind, k):
         self.kind = kind
-        if kind == "down":
+        if kind in ("half", "down"):
             q = k - N_LAYER
             per = FF // PIECE
             self.width = PIECE
@@ -61,7 +62,12 @@
             self.j = 6 if kind == "embed" else (k - N_EMBED) // BLOCK
         self.row = pl.multiple_of((q // per) * 8, 8)
         self.rows = pl.ds(self.row, 8)
-        self.cols = pl.ds(pl.multiple_of((q % per) * self.width, 512), self.width)
+        self.col = (q % per) * self.width
+        self.cols = pl.ds(pl.multiple_of(self.col, 512), self.width)
+
+    def half(self, dp):
+        half = self.width // 2
+        return pl.ds(pl.multiple_of(self.col + dp * half, 512), half)
 
     def source(self, grads, q):
         g_layer, g_down, g_embed = grads
@@ -80,7 +86,7 @@
         return down.at[self.rows, self.cols]
 
     def held(self, seven, down):
-        if self.kind == "down":
+        if self.kind in ("half", "down"):
             return down.at[self.rows, self.cols]
         return seven.at[self.j, self.rows, self.cols]
 
@@ -92,8 +98,8 @@
     if isinstance(k, int):
         use(Chunk("embed", k))
         return
-    bounds = (0, N_EMBED, N_LAYER, N)
-    for i, kind in enumerate(("embed", "layer", "down")):
+    bounds = (0, N_EMBED, N_LAYER, N_LAYER + N_HALF, N)
+    for i, kind in enumerate(("embed", "layer", "half", "down")):
         @pl.when(jnp.logical_and(k >= bounds[i], k < bounds[i + 1]))
         def _():
             use(Chunk(kind, k))
@@ -124,7 +130,7 @@
 def reduce_kernel(g_layer, g_down, g_norm, g_embed, layer_w, layer_m, layer_v, down_w, down_m, down_v,
                   norm_w, norm_m, norm_v, embed_w, embed_m, embed_v,
                   sq_out, g7, gd, gn, w7, m7, v7, wd, md, vd, wn, mn, vn,
-                  own_o, par_o, pm7, pmd, x7, xd, y7, yd, own_no, par_no, pmn, xn, yn, acc, sq_all, sq_first,
+                  own_o, par_o, pm7, pmd, x7, xd, y7, yd, own_no, par_no, pmn, xn, yn, acc, acc_first, sq_all, sq_first,
                   pre, fo_own, fo_par, f_held, f_y,
                   out_sem, other_sem, mine_sem, y_sem, st_sem, n_sem, sq_sem, f_sem, pre_sem, credit):
     dp = lax.axis_index("dp")
@@ -153,6 +159,18 @@
         sem = y_sem.at[lax.rem(k, Y_RING)]
         return remote(chunk.held(g7, gd), chunk.held(y7, yd), sem, sem, peer_y)
 
+    def half_copy(k, chunk):
+        sem = y_sem.at[lax.rem(k, Y_RING)]
+        give = chunk.half(1 - dp)
+        return remote(gd.at[chunk.rows, give], yd.at[chunk.rows, give], sem, sem, peer_y)
+
+    def by_core(chunk, on_whole, on_half):
+        if chunk.kind == "half":
+            pl.when(core == 0)(on_half)
+            pl.when(core == 1)(on_whole)
+        else:
+            on_whole()
+
     def push_other(k, chunk, source):
         s = lax.rem(k, RING)
         return remote(source, chunk.ring(par_o, s), out_sem.at[s], other_sem.at[s], peer_core)
@@ -215,7 +233,7 @@
 
     def start_y(k):
         def use(chunk):
-            y_copy(k, chunk).start()
+            by_core(chunk, lambda: y_copy(k, chunk).start(), lambda: half_copy(k, chunk).start())
             seven = chunk.kind in ("embed", "layer")
             for i, (src, dst) in enumerate((((layer_w, down_w, embed_w), (w7, wd)), ((layer_m, down_m, embed_m), (m7, md)),
                                             ((layer_v, down_v, embed_v), (v7, vd)))):
@@ -225,11 +243,23 @@
 
     def sum_y(k):
         def use(chunk):
-            take(times(2, chunk), y_sem.at[lax.rem(k, Y_RING)])
-            mine = chunk.held(g7, gd)
-            mean = (mine[...] + chunk.held(y7, yd)[...]) * 0.125
-            mine[...] = mean
-            acc[...] += squares(mean, chunk.width)
+            sem = y_sem.at[lax.rem(k, Y_RING)]
+
+            def whole():
+                take(times(2, chunk), sem)
+                mine = chunk.held(g7, gd)
+                mean = (mine[...] + chunk.held(y7, yd)[...]) * 0.125
+                mine[...] = mean
+                acc[...] += squares(mean, chunk.width)
+
+            def half():
+                take(times(1, chunk), sem)
+                keep = chunk.half(dp)
+                mean = (gd[chunk.rows, keep] + yd[chunk.rows, keep]) * 0.125
+                gd[chunk.rows, keep] = mean
+                acc_first[...] += squares(mean, chunk.width // 2)
+
+            by_core(chunk, whole, half)
 
         on_chunk(k, use)
 
@@ -258,6 +288,9 @@
                  remote(gd.at[last, give], yd.at[last, give], f_sem.at[6], f_sem.at[6], peer_y)]
     f_cross = remote(fo_own.at[:, keep_o], xd.at[last, keep], f_sem.at[7], f_sem.at[7], peer_x)
     f_gather = remote(gd.at[last, keep], yd.at[last, keep], f_sem.at[8], f_sem.at[8], peer_y)
+    halves = [Chunk("half", N_LAYER + i) for i in range(N_HALF)]
+    h_gather = [remote(gd.at[chunk.rows, chunk.half(dp)], yd.at[chunk.rows, chunk.half(dp)], f_sem.at[9], f_sem.at[9],
+                       peer_y) for chunk in halves]
     me = dp * 4 + f
     sqf_copies = [remote(sq_first.at[me], sq_first.at[me], sq_sem.at[0], sq_sem.at[1], peer)
                   for peer in peers]
@@ -284,6 +317,7 @@
     for copy in f_give + f_local:
         copy.start()
     acc[...] = jnp.zeros_like(acc)
+    acc_first[...] = jnp.zeros_like(acc_first)
 
     barrier = pltpu.get_barrier_semaphore()
     near = (peer_core, peer_x, peer_y)
@@ -291,9 +325,10 @@
         pl.semaphore_signal(barrier, inc=1, device_id=peer, device_id_type=MESH)
     take(f_held, f_sem.at[0])
     pl.semaphore_wait(barrier, len(near))
-    start(f_push[:2])
+    f_push[0].start()
     ahead.wait()
     push_other(0, zero, pre).start()
+    f_push[1].start()
     start(f_push[2:])
     push_mine(0, zero, zero.source(grads, f_core)).start()
     for k in range(1, FETCH - LEAD + 1):
@@ -302,11 +337,11 @@
     take(fo_par.at[:, give_o], f_sem.at[3])
     fo_own[:, give_o] = fo_own[:, give_o] + fo_par[:, give_o]
     f_scatter[0].start()
+    sum_chip(0)
+    start_x(0)
     take(fo_par.at[:, give_o], f_sem.at[4])
     gd[last, give] = gd[last, give] + pmd[last, give]
     f_scatter[1].start()
-    sum_chip(0)
-    start_x(0)
     take(fo_par, f_sem.at[5])
     take(f_held, f_sem.at[2])
     fo_own[:, keep_o] = fo_own[:, keep_o] + fo_par[:, keep_o]
@@ -360,12 +395,16 @@
         def _():
             f_cross.start()
 
+        @pl.when(jnp.logical_and(i == N, core == 0))
+        def _():
+            start(h_gather)
+
         @pl.when(i == N + LAG - 3)
         def _():
             take(fo_par, f_sem.at[7])
             mean = (gd[last, keep] + xd[last, keep]) * 0.125
             gd[last, keep] = mean
-            sq_first[me] = squares(mean, SPLIT)
+            sq_first[me] = acc_first[...] + squares(mean, SPLIT)
             start(sqf_copies)
             f_gather.start()
 
@@ -387,6 +426,13 @@
     lax.fori_loop(N - RING, N, drain, 0)
     for i, ref in enumerate((w7, m7, v7, wd, md, vd)):
         pltpu.make_async_copy(ref, ref, st_sem.at[i]).wait()
+
+    @pl.when(core == 0)
+    def _():
+        take(gd.at[pl.ds(0, 8), pl.ds(0, N_HALF * PIECE)], f_sem.at[9])
+        for chunk in halves:
+            gd[chunk.rows, chunk.half(1 - dp)] = yd[chunk.rows, chunk.half(1 - dp)]
+
     take(fo_par, f_sem.at[8])
     gd[last, give] = yd[last, give]
     take(sq_first.at[pl.ds(0, 7)], sq_sem.at[0])
@@ -514,10 +560,10 @@
         scratch_shapes=[pltpu.VMEM((RING, 8, max(PART, PIECE)), F32)] * 2
         + [pltpu.VMEM(SEVEN, F32), pltpu.VMEM(DOWN, F32)] * 3
         + [pltpu.VMEM(NORM, F32)] * 5
-        + [pltpu.VMEM((8, 128), F32), pltpu.VMEM((4, 8, 128), F32), pltpu.VMEM((8, 8, 128), F32)]
+        + [pltpu.VMEM((8, 128), F32)] * 2 + [pltpu.VMEM((4, 8, 128), F32), pltpu.VMEM((8, 8, 128), F32)]
         + [pltpu.VMEM((8, PART), F32)] + [pltpu.VMEM((FIRST, FIRST_COLS), F32)] * 2
         + [pltpu.VMEM((2, FIRST, FIRST_COLS), F32), pltpu.VMEM((FIRST, SPLIT), F32)]
-        + [dma((RING,)), dma((RING,)), dma((M_RING,)), dma((Y_RING,)), dma((6,)), dma((4,)), dma((4,)), dma((9,)), dma,
+        + [dma((RING,)), dma((RING,)), dma((M_RING,)), dma((Y_RING,)), dma((6,)), dma((4,)), dma((4,)), dma((10,)), dma,
            pltpu.SemaphoreType.REGULAR],
         compiler_params=pltpu.CompilerParams(collective_id=0, has_side_effects=True,
                                              vmem_limit_bytes=26 * 1024 * 1024),

time: 183 us -> 183 us (level)
  no operation moved by 1% of the time
where the time goes in v8:
time: 183 us
  Pallas kernels  182 us (99%)
    pallas_call x1, Pallas kernels, local_update(): pl.pallas_call(reduce_kernel, out_shape=[pltpu.VMEM(shape, F32) for shape...  173 us
    pallas_call x1, Pallas kernels, local_update(): pl.pallas_call(update_kernel, out_shape=out_shape, in_specs=[vmem_spec] *...  9.17 us

profile of v8, /device:TPU:0, one launch (start us, length us, event | category | flops | bytes accessed | tf_op | source)
XLA Modules:
  0.0 183.0 jit_solution(12955530382067294589)
XLA Ops:
  0.7 173.2 %shard_map.279 = (f32[8,128]{1,0:T(8,128)S(1)}, f32[7,64,3072]{2,1,0:T(8,128)S(1)}, f32[64,8192]{1,0:T(8,128)S(1)}, f32[4,768]{1,0:T(4,128)S(1)}, f32[7,64,3072]...) custom-call(f32[1,6,256,3072]{3,2,1,0:T(8,128)} %g_layer.1, ...), custom_call_target="tpu_custom_call" | custom-call | tf_op jit(solution)/shard_map/pallas_call | solution.py:555
  173.9 9.2 %shard_map.280 = (f32[6,64,3072]{2,1,0:T(8,128)}, f32[6,64,3072]{2,1,0:T(8,128)}, f32[6,64,3072]{2,1,0:T(8,128)}, bf16[6,64,3072]{2,1,0:T(8,128)(2,1)}, f32[64,8...) custom-call(f32[8,128]{1,0:T(8,128)S(1)} %get-tuple-element.29.sq, ...), custom_call_target="tpu_custom_call" | custom-call | tf_op jit(solution)/shard_map/pallas_call | solution.py:575

commit v9 on v8

--- a/solution.py
+++ b/solution.py
@@ -404,7 +404,7 @@
             take(fo_par, f_sem.at[7])
             mean = (gd[last, keep] + xd[last, keep]) * 0.125
             gd[last, keep] = mean
-            sq_first[me] = acc_first[...] + squares(mean, SPLIT)
+            sq_first[me] = jnp.sum(acc_first[...] + squares(mean, SPLIT), axis=0, keepdims=True)
             start(sqf_copies)
             f_gather.start()
 
@@ -413,7 +413,7 @@
 
     lax.fori_loop(FETCH - LEAD + 1, FETCH + N + LAG, step, 0)
 
-    sq_all[f] = acc[...]
+    sq_all[f] = jnp.sum(acc[...], axis=0, keepdims=True)
     copies = [remote(sq_all.at[f], sq_all.at[f], sq_sem.at[2], sq_sem.at[3], peer)
               for peer in (peer_core, peer_x, peer_diag)]
     for copy in copies:
@@ -551,7 +551,7 @@
     any_spec = pl.BlockSpec(memory_space=pl.ANY)
     vmem_spec = pl.BlockSpec(memory_space=pltpu.VMEM)
     dma = pltpu.SemaphoreType.DMA
-    held = [(8, 128)] + [SEVEN, DOWN, NORM] + [SEVEN] * 3 + [DOWN] * 3 + [NORM] * 3
+    held = [(1, 128)] + [SEVEN, DOWN, NORM] + [SEVEN] * 3 + [DOWN] * 3 + [NORM] * 3
     reduced = pl.pallas_call(
         reduce_kernel,
         out_shape=[pltpu.VMEM(shape, F32) for shape in held],
@@ -560,7 +560,7 @@
         scratch_shapes=[pltpu.VMEM((RING, 8, max(PART, PIECE)), F32)] * 2
         + [pltpu.VMEM(SEVEN, F32), pltpu.VMEM(DOWN, F32)] * 3
         + [pltpu.VMEM(NORM, F32)] * 5
-        + [pltpu.VMEM((8, 128), F32)] * 2 + [pltpu.VMEM((4, 8, 128), F32), pltpu.VMEM((8, 8, 128), F32)]
+        + [pltpu.VMEM((8, 128), F32)] * 2 + [pltpu.VMEM((4, 1, 128), F32), pltpu.VMEM((8, 1, 128), F32)]
         + [pltpu.VMEM((8, PART), F32)] + [pltpu.VMEM((FIRST, FIRST_COLS), F32)] * 2
         + [pltpu.VMEM((2, FIRST, FIRST_COLS), F32), pltpu.VMEM((FIRST, SPLIT), F32)]
         + [dma((RING,)), dma((RING,)), dma((M_RING,)), dma((Y_RING,)), dma((6,)), dma((4,)), dma((4,)), dma((10,)), dma,

time: 183 us -> 183 us (level)
  no operation moved by 1% of the time
where the time goes in v9:
time: 183 us
  Pallas kernels  182 us (99%)
    pallas_call x1, Pallas kernels, local_update(): pl.pallas_call(reduce_kernel, out_shape=[pltpu.VMEM(shape, F32) for shape...  173 us
    pallas_call x1, Pallas kernels, local_update(): pl.pallas_call(update_kernel, out_shape=out_shape, in_specs=[vmem_spec] *...  9.17 us

profile of v9, /device:TPU:0, one launch (start us, length us, event | category | flops | bytes accessed | tf_op | source)
XLA Modules:
  0.0 182.8 jit_solution(10682349174572689755)
XLA Ops:
  0.7 173.0 %shard_map.279 = (f32[1,128]{1,0:T(1,128)S(1)}, f32[7,64,3072]{2,1,0:T(8,128)S(1)}, f32[64,8192]{1,0:T(8,128)S(1)}, f32[4,768]{1,0:T(4,128)S(1)}, f32[7,64,3072]...) custom-call(f32[1,6,256,3072]{3,2,1,0:T(8,128)} %g_layer.1, ...), custom_call_target="tpu_custom_call" | custom-call | tf_op jit(solution)/shard_map/pallas_call | solution.py:555
  173.7 9.2 %shard_map.280 = (f32[6,64,3072]{2,1,0:T(8,128)}, f32[6,64,3072]{2,1,0:T(8,128)}, f32[6,64,3072]{2,1,0:T(8,128)}, bf16[6,64,3072]{2,1,0:T(8,128)(2,1)}, f32[64,8...) custom-call(f32[1,128]{1,0:T(1,128)S(1)} %get-tuple-element.29.sq, ...), custom_call_target="tpu_custom_call" | custom-call | tf_op jit(solution)/shard_map/pallas_call | solution.py:575

commit v10 on v9

--- a/solution.py
+++ b/solution.py
@@ -42,7 +42,7 @@
 
 LEAD = 5
 FETCH = 7
-RING = 9
+RING = 8
 LAG = 5
 Y_RING = 2 * LAG + 2
 M_RING = RING + LEAD
@@ -309,6 +309,10 @@
         return fo_par.at[:, pl.ds(0, count * NORM[0] * NORM[1] // 8)]
 
 
+    barrier = pltpu.get_barrier_semaphore()
+    near = (peer_core, peer_x, peer_y)
+    for peer in near:
+        pl.semaphore_signal(barrier, inc=1, device_id=peer, device_id_type=MESH)
     zero = Chunk("embed", 0)
     ahead = pltpu.make_async_copy(zero.source(grads, f_diag), pre, pre_sem)
     ahead.start()
@@ -319,10 +323,6 @@
     acc[...] = jnp.zeros_like(acc)
     acc_first[...] = jnp.zeros_like(acc_first)
 
-    barrier = pltpu.get_barrier_semaphore()
-    near = (peer_core, peer_x, peer_y)
-    for peer in near:
-        pl.semaphore_signal(barrier, inc=1, device_id=peer, device_id_type=MESH)
     take(f_held, f_sem.at[0])
     pl.semaphore_wait(barrier, len(near))
     f_push[0].start()
@@ -405,8 +405,8 @@
             mean = (gd[last, keep] + xd[last, keep]) * 0.125
             gd[last, keep] = mean
             sq_first[me] = jnp.sum(acc_first[...] + squares(mean, SPLIT), axis=0, keepdims=True)
+            f_gather.start()
             start(sqf_copies)
-            f_gather.start()
 
         sum_y(i - LAG)
         return 0
@@ -526,8 +526,7 @@
         return 0
 
     lax.fori_loop(0, 4, first_step, 0)
-    lax.fori_loop(0, 2, half_step, 0)
-    lax.fori_loop(2, 6, layer_step, 0)
+    lax.fori_loop(1, 6, layer_step, 0)
     out = update_math(*scales, gn[...], wn[...], mn[...], vn[...], WEIGHT_DECAY)
     for ref, val in zip((snw, snm, snv, snb), out):
         ref[...] = val

time: 183 us -> 183 us (level)
  no operation moved by 1% of the time
where the time goes in v10:
time: 183 us
  Pallas kernels  182 us (99%)
    pallas_call x1, Pallas kernels, local_update(): pl.pallas_call(reduce_kernel, out_shape=[pltpu.VMEM(shape, F32) for shape...  173 us
    pallas_call x1, Pallas kernels, local_update(): pl.pallas_call(update_kernel, out_shape=out_shape, in_specs=[vmem_spec] *...  9.16 us

profile of v10, /device:TPU:0, one launch (start us, length us, event | category | flops | bytes accessed | tf_op | source)
XLA Modules:
  0.0 182.8 jit_solution(4483282912927756361)
XLA Ops:
  0.7 173.0 %shard_map.279 = (f32[1,128]{1,0:T(1,128)S(1)}, f32[7,64,3072]{2,1,0:T(8,128)S(1)}, f32[64,8192]{1,0:T(8,128)S(1)}, f32[4,768]{1,0:T(4,128)S(1)}, f32[7,64,3072]...) custom-call(f32[1,6,256,3072]{3,2,1,0:T(8,128)} %g_layer.1, ...), custom_call_target="tpu_custom_call" | custom-call | tf_op jit(solution)/shard_map/pallas_call | solution.py:554
  173.6 9.2 %shard_map.280 = (f32[6,64,3072]{2,1,0:T(8,128)}, f32[6,64,3072]{2,1,0:T(8,128)}, f32[6,64,3072]{2,1,0:T(8,128)}, bf16[6,64,3072]{2,1,0:T(8,128)(2,1)}, f32[64,8...) custom-call(f32[1,128]{1,0:T(1,128)S(1)} %get-tuple-element.29.sq, ...), custom_call_target="tpu_custom_call" | custom-call | tf_op jit(solution)/shard_map/pallas_call | solution.py:574

commit v11 on v10

--- a/solution.py
+++ b/solution.py
@@ -237,7 +237,7 @@
             seven = chunk.kind in ("embed", "layer")
             for i, (src, dst) in enumerate((((layer_w, down_w, embed_w), (w7, wd)), ((layer_m, down_m, embed_m), (m7, md)),
                                             ((layer_v, down_v, embed_v), (v7, vd)))):
-                pltpu.make_async_copy(chunk.state(*src), chunk.held(*dst), st_sem.at[i if seven else 3 + i]).start()
+                pltpu.make_async_copy(chunk.state(*src), chunk.held(*dst), st_sem.at[0 if seven else 1]).start()
 
         on_chunk(k, use)
 
@@ -282,7 +282,7 @@
         for i, ref in enumerate((fo_par.at[:, half_o], pmd.at[last, half])):
             f_push.append(remote(f_held.at[i, :, half_o], ref, f_sem.at[2],
                                  f_sem.at[3 + i] if h == 0 else f_sem.at[5], peer_core))
-    f_state = [pltpu.make_async_copy(src.at[last, cols], dst.at[last, cols], st_sem.at[3 + i])
+    f_state = [pltpu.make_async_copy(src.at[last, cols], dst.at[last, cols], st_sem.at[1])
                for i, (src, dst) in enumerate(((down_w, wd), (down_m, md), (down_v, vd)))]
     f_scatter = [remote(fo_own.at[:, give_o], f_y, f_sem.at[6], f_sem.at[6], peer_y),
                  remote(gd.at[last, give], yd.at[last, give], f_sem.at[6], f_sem.at[6], peer_y)]
@@ -425,7 +425,7 @@
 
     lax.fori_loop(N - RING, N, drain, 0)
     for i, ref in enumerate((w7, m7, v7, wd, md, vd)):
-        pltpu.make_async_copy(ref, ref, st_sem.at[i]).wait()
+        pltpu.make_async_copy(ref, ref, st_sem.at[i // 3]).wait()
 
     @pl.when(core == 0)
     def _():
@@ -468,16 +468,16 @@
 
     def layer_copies(j, row, rows):
         at = pl.ds(row, rows)
-        return [pltpu.make_async_copy(src.at[j, at, :], dst.at[j, at, :], sem.at[0, a])
+        return [pltpu.make_async_copy(src.at[j, at, :], dst.at[j, at, :], sem.at[0, a // 3])
                 for a, (src, dst) in enumerate(zip(seven_staged, outs[0]))]
 
     def embed_copies():
-        return [pltpu.make_async_copy(src.at[6], dst, sem.at[1, a])
+        return [pltpu.make_async_copy(src.at[6], dst, sem.at[1, a // 3])
                 for a, (src, dst) in enumerate(zip(seven_staged, outs[3]))]
 
     def down_copies(t):
         at = pl.ds(pl.multiple_of(t * 16, 16), 16)
-        return [pltpu.make_async_copy(src.at[at, :], dst.at[at, :], sem.at[2, a])
+        return [pltpu.make_async_copy(src.at[at, :], dst.at[at, :], sem.at[2, a // 3])
                 for a, (src, dst) in enumerate(zip(down_staged, outs[1]))]
 
     def seven(j, row, decay):
@@ -530,7 +530,7 @@
     out = update_math(*scales, gn[...], wn[...], mn[...], vn[...], WEIGHT_DECAY)
     for ref, val in zip((snw, snm, snv, snb), out):
         ref[...] = val
-    norm_copies = [pltpu.make_async_copy(src, dst, sem.at[3, a])
+    norm_copies = [pltpu.make_async_copy(src, dst, sem.at[3, a // 3])
                    for a, (src, dst) in enumerate(zip((snw, snm, snv, snb), outs[2]))]
     start(norm_copies)
     block(6, 0.0)
@@ -538,11 +538,11 @@
     lax.fori_loop(0, 4, down_step, 0)
 
     for a, staged in enumerate(seven_staged):
-        pltpu.make_async_copy(staged.at[pl.ds(0, 6)], outs[0][a], sem.at[0, a]).wait()
+        pltpu.make_async_copy(staged.at[pl.ds(0, 6)], outs[0][a], sem.at[0, a // 3]).wait()
     wait(embed_copies())
     wait(norm_copies)
     for a, staged in enumerate(down_staged):
-        pltpu.make_async_copy(staged, outs[1][a], sem.at[2, a]).wait()
+        pltpu.make_async_copy(staged, outs[1][a], sem.at[2, a // 3]).wait()
 
 
 def local_update(g_layer, g_down, g_norm, g_embed, layer_w, layer_m, layer_v, down_w, down_m, down_v, norm_w, norm_m,
@@ -562,7 +562,7 @@
         + [pltpu.VMEM((8, 128), F32)] * 2 + [pltpu.VMEM((4, 1, 128), F32), pltpu.VMEM((8, 1, 128), F32)]
         + [pltpu.VMEM((8, PART), F32)] + [pltpu.VMEM((FIRST, FIRST_COLS), F32)] * 2
         + [pltpu.VMEM((2, FIRST, FIRST_COLS), F32), pltpu.VMEM((FIRST, SPLIT), F32)]
-        + [dma((RING,)), dma((RING,)), dma((M_RING,)), dma((Y_RING,)), dma((6,)), dma((4,)), dma((4,)), dma((10,)), dma,
+        + [dma((RING,)), dma((RING,)), dma((M_RING,)), dma((Y_RING,)), dma((2,)), dma((4,)), dma((4,)), dma((10,)), dma,
            pltpu.SemaphoreType.REGULAR],
         compiler_params=pltpu.CompilerParams(collective_id=0, has_side_effects=True,
                                              vmem_limit_bytes=26 * 1024 * 1024),
@@ -576,7 +576,7 @@
         out_shape=out_shape,
         in_specs=[vmem_spec] * len(held),
         out_specs=[any_spec] * 16,
-        scratch_shapes=staged + [dma((4, 4))],
+        scratch_shapes=staged + [dma((4, 2))],
         compiler_params=pltpu.CompilerParams(vmem_limit_bytes=26 * 1024 * 1024),
     )(*[pltpu.with_memory_space_constraint(a, pltpu.VMEM) for a in reduced])
 

time: 183 us -> 183 us (level)
  no operation moved by 1% of the time
where the time goes in v11:
time: 183 us
  Pallas kernels  182 us (99%)
    pallas_call x1, Pallas kernels, local_update(): pl.pallas_call(reduce_kernel, out_shape=[pltpu.VMEM(shape, F32) for shape...  173 us
    pallas_call x1, Pallas kernels, local_update(): pl.pallas_call(update_kernel, out_shape=out_shape, in_specs=[vmem_spec] *...  9.09 us

profile of v11, /device:TPU:0, one launch (start us, length us, event | category | flops | bytes accessed | tf_op | source)
XLA Modules:
  0.0 182.7 jit_solution(16826738058850692837)
XLA Ops:
  0.7 172.9 %shard_map.279 = (f32[1,128]{1,0:T(1,128)S(1)}, f32[7,64,3072]{2,1,0:T(8,128)S(1)}, f32[64,8192]{1,0:T(8,128)S(1)}, f32[4,768]{1,0:T(4,128)S(1)}, f32[7,64,3072]...) custom-call(f32[1,6,256,3072]{3,2,1,0:T(8,128)} %g_layer.1, ...), custom_call_target="tpu_custom_call" | custom-call | tf_op jit(solution)/shard_map/pallas_call | solution.py:554
  173.6 9.1 %shard_map.280 = (f32[6,64,3072]{2,1,0:T(8,128)}, f32[6,64,3072]{2,1,0:T(8,128)}, f32[6,64,3072]{2,1,0:T(8,128)}, bf16[6,64,3072]{2,1,0:T(8,128)(2,1)}, f32[64,8...) custom-call(f32[1,128]{1,0:T(1,128)S(1)} %get-tuple-element.29.sq, ...), custom_call_target="tpu_custom_call" | custom-call | tf_op jit(solution)/shard_map/pallas_call | solution.py:574

commit v12 on v11

--- a/solution.py
+++ b/solution.py
@@ -468,16 +468,16 @@
 
     def layer_copies(j, row, rows):
         at = pl.ds(row, rows)
-        return [pltpu.make_async_copy(src.at[j, at, :], dst.at[j, at, :], sem.at[0, a // 3])
+        return [pltpu.make_async_copy(src.at[j, at, :], dst.at[j, at, :], sem.at[0])
                 for a, (src, dst) in enumerate(zip(seven_staged, outs[0]))]
 
     def embed_copies():
-        return [pltpu.make_async_copy(src.at[6], dst, sem.at[1, a // 3])
+        return [pltpu.make_async_copy(src.at[6], dst, sem.at[0])
                 for a, (src, dst) in enumerate(zip(seven_staged, outs[3]))]
 
     def down_copies(t):
         at = pl.ds(pl.multiple_of(t * 16, 16), 16)
-        return [pltpu.make_async_copy(src.at[at, :], dst.at[at, :], sem.at[2, a // 3])
+        return [pltpu.make_async_copy(src.at[at, :], dst.at[at, :], sem.at[0])
                 for a, (src, dst) in enumerate(zip(down_staged, outs[1]))]
 
     def seven(j, row, decay):
@@ -530,7 +530,7 @@
     out = update_math(*scales, gn[...], wn[...], mn[...], vn[...], WEIGHT_DECAY)
     for ref, val in zip((snw, snm, snv, snb), out):
         ref[...] = val
-    norm_copies = [pltpu.make_async_copy(src, dst, sem.at[3, a // 3])
+    norm_copies = [pltpu.make_async_copy(src, dst, sem.at[0])
                    for a, (src, dst) in enumerate(zip((snw, snm, snv, snb), outs[2]))]
     start(norm_copies)
     block(6, 0.0)
@@ -538,11 +538,11 @@
     lax.fori_loop(0, 4, down_step, 0)
 
     for a, staged in enumerate(seven_staged):
-        pltpu.make_async_copy(staged.at[pl.ds(0, 6)], outs[0][a], sem.at[0, a // 3]).wait()
+        pltpu.make_async_copy(staged.at[pl.ds(0, 6)], outs[0][a], sem.at[0]).wait()
     wait(embed_copies())
     wait(norm_copies)
     for a, staged in enumerate(down_staged):
-        pltpu.make_async_copy(staged, outs[1][a], sem.at[2, a // 3]).wait()
+        pltpu.make_async_copy(staged, outs[1][a], sem.at[0]).wait()
 
 
 def local_update(g_layer, g_down, g_norm, g_embed, layer_w, layer_m, layer_v, down_w, down_m, down_v, norm_w, norm_m,
@@ -576,7 +576,7 @@
         out_shape=out_shape,
         in_specs=[vmem_spec] * len(held),
         out_specs=[any_spec] * 16,
-        scratch_shapes=staged + [dma((4, 2))],
+        scratch_shapes=staged + [dma((1,))],
         compiler_params=pltpu.CompilerParams(vmem_limit_bytes=26 * 1024 * 1024),
     )(*[pltpu.with_memory_space_constraint(a, pltpu.VMEM) for a in reduced])
 

time: 183 us -> 183 us (level)
  no operation moved by 1% of the time
where the time goes in v12:
time: 183 us
  Pallas kernels  182 us (99%)
    pallas_call x1, Pallas kernels, local_update(): pl.pallas_call(reduce_kernel, out_shape=[pltpu.VMEM(shape, F32) for shape...  173 us
    pallas_call x1, Pallas kernels, local_update(): pl.pallas_call(update_kernel, out_shape=out_shape, in_specs=[vmem_spec] *...  9.03 us

profile of v12, /device:TPU:0, one launch (start us, length us, event | category | flops | bytes accessed | tf_op | source)
XLA Modules:
  0.0 182.6 jit_solution(10610965572667334978)
XLA Ops:
  0.7 172.9 %shard_map.279 = (f32[1,128]{1,0:T(1,128)S(1)}, f32[7,64,3072]{2,1,0:T(8,128)S(1)}, f32[64,8192]{1,0:T(8,128)S(1)}, f32[4,768]{1,0:T(4,128)S(1)}, f32[7,64,3072]...) custom-call(f32[1,6,256,3072]{3,2,1,0:T(8,128)} %g_layer.1, ...), custom_call_target="tpu_custom_call" | custom-call | tf_op jit(solution)/shard_map/pallas_call | solution.py:554
  173.6 9.0 %shard_map.280 = (f32[6,64,3072]{2,1,0:T(8,128)}, f32[6,64,3072]{2,1,0:T(8,128)}, f32[6,64,3072]{2,1,0:T(8,128)}, bf16[6,64,3072]{2,1,0:T(8,128)(2,1)}, f32[64,8...) custom-call(f32[1,128]{1,0:T(1,128)S(1)} %get-tuple-element.29.sq, ...), custom_call_target="tpu_custom_call" | custom-call | tf_op jit(solution)/shard_map/pallas_call | solution.py:574
